TPU v7x, 16 devices: a whole 2x2x2 slice. The times are simulated.
16 devices in a mesh: dp: 4 (over z, y), ep: 4 (over x, core).
Axes of the slice: x: 2, y: 2, z: 2, core: 2. Of those that a mesh axis runs over, the one named last changes fastest.
Arguments:
- x_rows: bfloat16 [4096, 2048], P(('dp', 'ep')), parts along dimension 0
- logits: float32 [4096, 64], P(('dp', 'ep')), parts along dimension 0
- w_in: bfloat16 [64, 2048, 1408], P('ep')
- w_out: bfloat16 [64, 1408, 2048], P('ep')
Outputs:
- output: bfloat16 [4096, 2048], P(('dp', 'ep')), parts along dimension 0
There are 4 independent parts. A program takes and returns all parts, laid end to end along the dimension named above; an argument that names none is the same for every part.
All inputs are finite; a program needn't handle non-finite values.
Results may differ from a plain program's by a relative error of at most 0.001.
Values are sent between devices in bfloat16 or wider.
A program may use at most 1 GiB of HBM per device.

v0:
```python
import jax
import jax.numpy as jnp
from jax import lax
from jax.sharding import PartitionSpec as P

CAP_FACTOR = 2


def solution(mesh):
    group_size = mesh.shape['ep']
    row_spec = P(('dp', 'ep'), None)
    expert_spec = P('ep', None, None)

    def local_step(x_rows, logits, w_in, w_out):
        tok_dev, d_model = x_rows.shape
        experts = logits.shape[1]
        exp_dev = w_in.shape[0]
        capacity = CAP_FACTOR * tok_dev * group_size // experts
        src_cap = 4 * tok_dev // experts
        my_index = lax.axis_index('ep')
        gate_probs = jax.nn.softmax(logits, axis=-1)
        top_vals, top_ids = lax.top_k(logits, 2)
        chosen = (logits >= top_vals[:, 1:2]).astype(jnp.int32)
        local_before = jnp.cumsum(chosen, axis=0) - chosen
        local_counts = jnp.sum(chosen, axis=0).astype(jnp.float32)
        all_counts = lax.all_gather(local_counts, 'ep').astype(jnp.int32)
        dev_offsets = jnp.cumsum(all_counts, axis=0) - all_counts
        local_pos = jnp.take_along_axis(local_before, top_ids, axis=1)
        kept_mask = local_pos + jnp.take(dev_offsets[my_index], top_ids) < capacity
        send_row = jnp.where(kept_mask, top_ids * src_cap + local_pos, experts * src_cap)
        tok_ids = jnp.broadcast_to(jnp.arange(tok_dev, dtype=jnp.int32)[:, None], (tok_dev, 2))
        slot_tok = jnp.full((experts * src_cap,), tok_dev, jnp.int32).at[send_row.reshape(-1)].set(tok_ids.reshape(-1), mode='drop')
        send_buf = jnp.take(x_rows, slot_tok, axis=0, mode='fill', fill_value=0)
        recv_buf = lax.all_to_all(send_buf, 'ep', 0, 0, tiled=True)

        own_counts = lax.dynamic_slice_in_dim(all_counts, my_index * exp_dev, exp_dev, axis=1)
        own_offsets = lax.dynamic_slice_in_dim(dev_offsets, my_index * exp_dev, exp_dev, axis=1)
        kept_counts = jnp.minimum(jnp.maximum(capacity - own_offsets, 0), own_counts)
        slot_ends = (own_offsets + kept_counts).T
        cap_ids = jnp.arange(capacity, dtype=jnp.int32)
        below_mask = slot_ends[:, None, :] <= cap_ids[None, :, None]
        src_dev = jnp.sum(below_mask.astype(jnp.int32), axis=2)
        slot_start = jnp.sum(jnp.where(below_mask, kept_counts.T[:, None, :], 0), axis=2)
        exp_local = jnp.arange(exp_dev, dtype=jnp.int32)
        recv_row = (src_dev * exp_dev + exp_local[:, None]) * src_cap + cap_ids[None, :] - slot_start
        recv_row = jnp.where(src_dev < group_size, recv_row, group_size * exp_dev * src_cap)
        expert_rows = jnp.take(recv_buf, recv_row.reshape(-1), axis=0, mode='fill', fill_value=0).reshape(exp_dev, capacity, d_model)
        hidden = jax.nn.gelu(jnp.einsum('ecd,edf->ecf', expert_rows, w_in, preferred_element_type=jnp.float32), approximate=True).astype(jnp.bfloat16)
        expert_out = jnp.einsum('ecf,efd->ecd', hidden, w_out, preferred_element_type=jnp.float32).astype(jnp.bfloat16).reshape(exp_dev * capacity, d_model)

        src_slots = jnp.arange(src_cap, dtype=jnp.int32)
        back_row = exp_local[None, :, None] * capacity + own_offsets[:, :, None] + src_slots[None, None, :]
        back_row = jnp.where(src_slots[None, None, :] < kept_counts[:, :, None], back_row, exp_dev * capacity)
        back_buf = jnp.take(expert_out, back_row.reshape(-1), axis=0, mode='fill', fill_value=0)
        ret_buf = lax.all_to_all(back_buf, 'ep', 0, 0, tiled=True)

        rows_back = jnp.take(ret_buf, send_row, axis=0, mode='fill', fill_value=0)
        pick_gate = jnp.take_along_axis(gate_probs, top_ids, axis=1)
        mix_sum = jnp.sum(pick_gate[:, :, None] * rows_back.astype(jnp.float32), axis=1)
        return (x_rows.astype(jnp.float32) + mix_sum).astype(jnp.bfloat16)

    return jax.shard_map(local_step, mesh=mesh, in_specs=(row_spec, row_spec, expert_spec, expert_spec), out_specs=row_spec, check_vma=False)
```

profile of v0, /device:TPU:0, one launch (start us, length us, event | category | flops | bytes accessed | tf_op | source)
XLA Modules:
  0.0 246.6 jit_solution(5199505840474184734)
XLA Ops:
  0.0 1.8 top_k.11
  1.9 0.9 convert_bitcast_fusion
  2.7 0.6 reduce-window.6
  3.6 1.2 dynamic-slice
  5.7 8.6 %all-reduce = f32[256]{0:T(256)S(1)} all-reduce(f32[256]{0:T(256)S(1)} %convert_dynamic-update-slice_fusion), channel_id=2, replica_groups=mesh['dp'=4,'ep'=4] {'ep'}, use_global_device_ids=true, to_apply=%add | all-reduce | flops 256 | bytes 2048
  14.8 3.3 %gather_fusion = s32[512]{0:T(512)S(1)} fusion(s32[64]{0:T(128)S(1)} %fusion.19, s32[1024]{0:T(1024)S(1)} %pad_clamp_fusion.2), kind=kCustom, calls=%fused_computation | custom fusion | bytes 6144 | tf_op jit(solution)/shard_map/jit(_take)/gather | solution.py:29
  18.6 4.5 %gather_fusion.6 = s32[512]{0:T(512)S(1)} fusion(s32[256,64]{0,1:T(8,128)S(1)} %get-tuple-element.21, s32[512]{0:T(512)S(1)} %reshape.326), kind=kCustom, calls=%fused_computation.6 | custom fusion | bytes 8192 | tf_op jit(solution)/shard_map/jit(take_along_axis)/gather | solution.py:28
  23.9 2.4 scatter_custom_fusion
  26.4 6.0 %gather_fusion.1 = bf16[1024,2048]{1,0:T(8,128)(2,1)} fusion(bf16[256,2048]{1,0:T(8,128)(2,1)S(1)} %copy-done, s32[1024]{0:T(1024)S(1)} %fusion.16), kind=kCustom, calls=%fused_computation.1 | custom fusion | bytes 8392704 | tf_op jit(solution)/shard_map/jit(_take)/gather | solution.py:33
  32.4 4.5 %broadcast_select_fusion = bf16[4,256,2048]{2,1,0:T(8,128)(2,1)} fusion(bf16[4,256,2048]{2,1,0:T(8,128)(2,1)} %bitcast.42, pred[4,256]{1,0:T(4,128)(4,1)S(1)} %broadcast_in_dim.120), kind=kLoop, calls=%fused_computation.10 | loop fusion | flops 2097152 | bytes 8389632 | tf_op jit(solution)/shard_map/jit(_take)/select_n | solution.py:33
  36.9 5.0 %all-to-all-start = ((bf16[4,256,2048]{2,1,0:T(8,128)(2,1)}), bf16[4,256,2048]{2,1,0:T(8,128)(2,1)}, u32[]{:S(2)}, u32[]{:S(2)}) async-start(bf16[4,256,2048]{2,1,0:T(8,128)(2,1)} %broadcast_select_fusion), calls=%async_computation | async-start | bytes 8388608 | tf_op jit(solution)/shard_map/all_to_all | solution.py:34
  42.6 47.1 %all-to-all-done = bf16[4,256,2048]{2,1,0:T(8,128)(2,1)} async-done(((bf16[4,256,2048]{2,1,0:T(8,128)(2,1)}), bf16[4,256,2048]{2,1,0:T(8,128)(2,1)}, u32[]{:S(2)}, u32[]{:S(2)}) %all-to-all-start) | async-done | bytes 4194336 | tf_op jit(solution)/shard_map/all_to_all | solution.py:34
  89.7 7.1 %gather_fusion.2 = bf16[512,2048]{1,0:T(8,128)(2,1)S(1)} fusion(bf16[1024,2048]{1,0:T(8,128)(2,1)} %bitcast.10, s32[1024]{0:T(1024)S(1)} %pad_clamp_fusion.1), kind=kCustom, calls=%fused_computation.2 | custom fusion | bytes 4196352 | tf_op jit(solution)/shard_map/jit(_take)/gather | solution.py:47
  96.8 33.6 %fusion.7 = bf16[16,32,1408]{2,1,0:T(8,128)(2,1)} fusion(bf16[16,2048,1408]{2,1,0:T(8,128)(2,1)} %param.6, bf16[16,32,2048]{2,1,0:T(8,128)(2,1)S(1)} %bitcast.43, pred[16,32]{1,0:T(8,128)(4,1)S(1)} %get-tuple-element.15), kind=kOutput, calls=%fused_computation.21 | convolution fusion | flops 2960326656 | bytes 95814144 | tf_op jit(solution)/shard_map/ecd,edf->ecf/dot_general | solution.py:48
  130.3 31.9 %convolution_convert_fusion = bf16[16,32,2048]{2,1,0:T(8,128)(2,1)S(1)} fusion(bf16[16,32,1408]{2,1,0:T(8,128)(2,1)} %fusion.7, bf16[16,1408,2048]{2,1,0:T(8,128)(2,1)} %param.7), kind=kOutput, calls=%fused_computation.13 | convolution fusion | flops 2953838592 | bytes 95813632 | tf_op jit(solution)/shard_map/ecf,efd->ecd/dot_general | solution.py:49
  162.2 6.0 %gather_fusion.3 = bf16[1024,2048]{1,0:T(8,128)(2,1)} fusion(bf16[512,2048]{1,0:T(8,128)(2,1)S(1)} %bitcast.40, s32[1024]{0:T(1024)S(1)} %broadcast_clamp_fusion), kind=kCustom, calls=%fused_computation.3 | custom fusion | bytes 8392704 | tf_op jit(solution)/shard_map/jit(_take)/gather | solution.py:54
  168.2 4.5 %broadcast_select_fusion.1 = bf16[4,256,2048]{2,1,0:T(8,128)(2,1)} fusion(bf16[4,256,2048]{2,1,0:T(8,128)(2,1)} %bitcast.41, pred[4,256]{1,0:T(4,128)(4,1)S(1)} %compare_and_fusion.2), kind=kLoop, calls=%fused_computation.11 | loop fusion | flops 2097152 | bytes 8389632 | tf_op jit(solution)/shard_map/jit(_take)/select_n | solution.py:54
  172.7 5.2 %all-to-all-start.1 = ((bf16[4,256,2048]{2,1,0:T(8,128)(2,1)}), bf16[4,256,2048]{2,1,0:T(8,128)(2,1)}, u32[]{:S(2)}, u32[]{:S(2)}) async-start(bf16[4,256,2048]{2,1,0:T(8,128)(2,1)} %broadcast_select_fusion.1), calls=%async_computation.1 | async-start | bytes 8388608 | tf_op jit(solution)/shard_map/all_to_all | solution.py:55
  178.5 4.5 %gather_fusion.5 = f32[512]{0:T(512)S(1)} fusion(f32[256,64]{0,1:T(8,128)S(1)} %fusion.14, s32[512]{0:T(512)S(1)} %reshape.326), kind=kCustom, calls=%fused_computation.5 | custom fusion | bytes 8192 | tf_op jit(solution)/shard_map/jit(take_along_axis)/gather | solution.py:58
  183.5 42.1 %all-to-all-done.1 = bf16[4,256,2048]{2,1,0:T(8,128)(2,1)} async-done(((bf16[4,256,2048]{2,1,0:T(8,128)(2,1)}), bf16[4,256,2048]{2,1,0:T(8,128)(2,1)}, u32[]{:S(2)}, u32[]{:S(2)}) %all-to-all-start.1) | async-done | bytes 4194336 | tf_op jit(solution)/shard_map/all_to_all | solution.py:55
  225.6 7.1 %gather_fusion.4 = bf16[512,2048]{1,0:T(8,128)(2,1)S(1)} fusion(bf16[1024,2048]{1,0:T(8,128)(2,1)} %bitcast.16, s32[1024]{0:T(1024)S(1)} %pad_clamp_fusion), kind=kCustom, calls=%fused_computation.4 | custom fusion | bytes 4196352 | tf_op jit(solution)/shard_map/jit(_take)/gather | solution.py:57
  232.7 2.7 %reshape.319 = bf16[256,2,2048]{2,1,0:T(2,128)(2,1)} reshape(bf16[512,2048]{1,0:T(8,128)(2,1)S(1)} %gather_fusion.4) | data formatting | bytes 4194304 | tf_op jit(solution)/shard_map/jit(_take)/gather | solution.py:57
  235.4 9.9 %multiply_reduce_fusion = f32[256,2048]{1,0:T(8,128)S(1)} fusion(bf16[256,2,2048]{2,1,0:T(2,128)(2,1)} %reshape.319, pred[256,2]{1,0:T(8,128)(4,1)S(1)} %copy.29, f32[256,2]{1,0:T(8,128)S(1)} %copy.23), kind=kLoop, calls=%fused_computation.9 | loop fusion | flops 3670016 | bytes 4196864 | tf_op jit(solution)/shard_map/reduce_sum | solution.py:59
  245.3 1.3 add_convert_fusion
  (63 shorter events, 3.6 us)
Async XLA Ops:
  18.6 7.8 %copy-start = (bf16[256,2048]{1,0:T(8,128)(2,1)S(1)}, bf16[256,2048]{1,0:T(8,128)(2,1)}, u32[]{:S(2)}) copy-start(bf16[256,2048]{1,0:T(8,128)(2,1)} %param.4) | copy-start | bytes 3145732
  36.9 52.7 %all-to-all-start = ((bf16[4,256,2048]{2,1,0:T(8,128)(2,1)}), bf16[4,256,2048]{2,1,0:T(8,128)(2,1)}, u32[]{:S(2)}, u32[]{:S(2)}) async-start(bf16[4,256,2048]{2,1,0:T(8,128)(2,1)} %broadcast_select_fusion), calls=%async_computation | async-start | bytes 8388608 | tf_op jit(solution)/shard_map/all_to_all | solution.py:34
  172.7 5.7 %copy-start.1 = (f32[256,64]{0,1:T(8,128)S(1)}, f32[256,64]{0,1:T(8,128)}, u32[]{:S(2)}) copy-start(f32[256,64]{0,1:T(8,128)} %param.5) | copy-start | bytes 196612
  172.7 52.9 %all-to-all-start.1 = ((bf16[4,256,2048]{2,1,0:T(8,128)(2,1)}), bf16[4,256,2048]{2,1,0:T(8,128)(2,1)}, u32[]{:S(2)}, u32[]{:S(2)}) async-start(bf16[4,256,2048]{2,1,0:T(8,128)(2,1)} %broadcast_select_fusion.1), calls=%async_computation.1 | async-start | bytes 8388608 | tf_op jit(solution)/shard_map/all_to_all | solution.py:55
where the time goes:
time: 247 us
  waiting for transfers between devices  89.2 us (36%)
  matrix products  65.4 us (26%)
  local copies, waits for them, and re-layouts  47.9 us (19%)
  other arithmetic  24.2 us (10%)
  starting transfers between devices  10.2 us (4%)
  blocking collectives  8.6 us (3%)
    all_to_all x1, waiting for transfers between devices, local_step(): recv_buf = lax.all_to_all(send_buf, 'ep', 0, 0, tiled=True)  47.1 us
    all_to_all x1, waiting for transfers between devices, local_step(): ret_buf = lax.all_to_all(back_buf, 'ep', 0, 0, tiled=True)  42.1 us
    dot_general x1, matrix products, local_step(): jnp.einsum('ecd,edf->ecf', expert_rows, w_in, preferred_element_type=jnp....  33.6 us
    dot_general x1, matrix products, local_step(): jnp.einsum('ecf,efd->ecd', hidden, w_out, preferred_element_type=jnp.floa...  31.9 us
    reduce_sum x1, other arithmetic, local_step(): jnp.sum(pick_gate[:, :, None] * rows_back.astype(jnp.float32), axis=1)  9.9 us
    gather x2, local copies, waits for them, and re-layouts, local_step(): rows_back = jnp.take(ret_buf, send_row, axis=0, mode='fill', fill_value=0)  9.8 us
    unnamed x1, blocking collectives  8.6 us
    gather x1, local copies, waits for them, and re-layouts, local_step(): jnp.take(recv_buf, recv_row.reshape(-1), axis=0, mode='fill', fill_value=0)  7.13 us
  transfers between devices with their start and end apart: 2, of which 2 were waited for; matrix products, arithmetic and copies ran while one was open for 2% of the time, Pallas kernels for 0%

commit v1 on v0

v1 whole, which is shorter than its diff:
```python
import functools

import jax
import jax.numpy as jnp
from jax import lax
from jax.experimental import pallas as pl
from jax.experimental.pallas import tpu as pltpu
from jax.sharding import PartitionSpec as P

BF16 = jnp.bfloat16
F32 = jnp.float32
MESH = pl.DeviceIdType.MESH
NREL = 4
NCH = 4
NS1 = 12
NS2 = 3
PAIR = 2


def iota(shape, dim):
    return lax.broadcasted_iota(jnp.int32, shape, dim)


def moe_kernel(cap, x_hbm, logits_ref, w1_hbm, w2_hbm, out_ref, xall, st_own, st_all, dmat, xg, hacc, hb, w1buf, w2buf,
               zs, zr, acc, w1_sem, w2_sem, xl_sem, xs_sem, xr_sem, ss_sem, sr_sem, zs_sem, zr_sem):
    tok, nexp = logits_ref.shape
    edev, d_model, ff = w1_hbm.shape
    src_cap = xg.shape[2]
    slots = edev * src_cap
    ck = d_model // NCH
    rows = NREL * src_cap
    eblk = zr.shape[1] // rows
    nblk = edev // eblk

    me = lax.axis_index('ep')
    mx, mc = me // 2, me % 2
    dev = [me, 2 * mx + (1 - mc), 2 * (1 - mx) + mc, 2 * (1 - mx) + (1 - mc)]

    def w1_copy(i):
        c, e = i // edev, i % edev
        k = pl.multiple_of(c * ck, ck)
        s = i % NS1
        return pltpu.make_async_copy(w1_hbm.at[e, pl.ds(k, ck), :], w1buf.at[s], w1_sem.at[s])

    def w2_copy(e):
        s = e % NS2
        return pltpu.make_async_copy(w2_hbm.at[e], w2buf.at[s], w2_sem.at[s])

    def x_local(c):
        return pltpu.make_async_copy(x_hbm.at[:, pl.ds(c * ck, ck)], xall.at[0, c], xl_sem.at[c])

    def x_remote(c, slot):
        src = xall.at[2 if slot == 3 else 0, c]
        return pltpu.make_async_remote_copy(src_ref=src, dst_ref=xall.at[slot, c], send_sem=xs_sem.at[slot - 1, c],
                                            recv_sem=xr_sem.at[slot - 1, c],
                                            device_id={'ep': dev[2 if slot == 2 else 1]}, device_id_type=MESH)

    def s_remote(r):
        first = pl.multiple_of(dev[r] * edev, edev)
        return pltpu.make_async_remote_copy(src_ref=st_own.at[pl.ds(first, edev), :], dst_ref=st_all.at[r],
                                            send_sem=ss_sem.at[r - 1], recv_sem=sr_sem.at[r - 1],
                                            device_id={'ep': dev[r]}, device_id_type=MESH)

    def z_remote(e, r):
        b, q = e // eblk, e % eblk
        first = pl.multiple_of(r * (eblk * src_cap) + q * src_cap, src_cap)
        return pltpu.make_async_remote_copy(src_ref=zs.at[e, pl.ds(r * src_cap, src_cap), :],
                                            dst_ref=zr.at[b, pl.ds(first, src_cap), :],
                                            send_sem=zs_sem.at[r - 1, b], recv_sem=zr_sem.at[r - 1, b],
                                            device_id={'ep': dev[r]}, device_id_type=MESH)

    def z_block(b, r):
        part = zr.at[b, pl.ds(r * eblk * src_cap, eblk * src_cap), :]
        return pltpu.make_async_remote_copy(src_ref=part, dst_ref=part, send_sem=zs_sem.at[r - 1, b],
                                            recv_sem=zr_sem.at[r - 1, b], device_id={'ep': dev[r]}, device_id_type=MESH)

    barrier = pltpu.get_barrier_semaphore()
    for r in range(1, NREL):
        pl.semaphore_signal(barrier, inc=1, device_id={'ep': dev[r]}, device_id_type=MESH)
    for c in range(NCH):
        x_local(c).start()

    def start_w1(i, carry):
        w1_copy(i).start()
        return carry
    lax.fori_loop(0, NS1, start_w1, 0)
    for e in range(NS2):
        w2_copy(e).start()

    pl.semaphore_wait(barrier, NREL - 1)
    x_local(0).wait()
    x_remote(0, 2).start()
    x_remote(0, 1).start()

    logits = logits_ref[...]
    lt = logits.T
    m1t = jnp.max(lt, axis=0, keepdims=True)
    m2t = jnp.max(jnp.where(lt == m1t, -jnp.inf, lt), axis=0, keepdims=True)
    chosen_t = lt >= m2t
    upper = (iota((tok, tok), 0) < iota((tok, tok), 1)).astype(F32).astype(BF16)
    before_t = jnp.dot(chosen_t.astype(F32).astype(BF16), upper, preferred_element_type=F32)
    st_own[...] = jnp.where(chosen_t, before_t, -1.0).astype(BF16)

    m1 = jnp.max(logits, axis=1, keepdims=True)
    is1 = logits == m1
    rest = jnp.where(is1, -jnp.inf, logits)
    m2 = jnp.max(rest, axis=1, keepdims=True)
    is2 = rest == m2
    lower = (iota((tok, tok), 1) < iota((tok, tok), 0)).astype(F32).astype(BF16)
    chosen = jnp.logical_or(is1, is2).astype(F32).astype(BF16)
    before = jnp.dot(lower, chosen, preferred_element_type=F32)
    slot_id = iota((tok, nexp), 1).astype(F32) * src_cap + before
    slot1 = jnp.sum(jnp.where(is1, slot_id, 0.0), axis=1, keepdims=True)
    slot2 = jnp.sum(jnp.where(is2, slot_id, 0.0), axis=1, keepdims=True)
    total = jnp.sum(jnp.exp(logits - m1), axis=1, keepdims=True)
    gate1 = 1.0 / total
    gate2 = jnp.exp(m2 - m1) / total

    for r in (2, 3, 1):
        s_remote(r).start()
    for c in range(1, NCH):
        x_local(c).wait()
        x_remote(c, 2).start()
        x_remote(c, 1).start()

    for r in range(1, NREL):
        s_remote(r).wait_recv()
    own_first = pl.multiple_of(me * edev, edev)
    pos = [st_own[pl.ds(own_first, edev), :].astype(F32)] + [st_all[r].astype(F32) for r in range(1, NREL)]
    cnt = [jnp.sum((p >= 0.0).astype(F32), axis=1, keepdims=True) for p in pos]
    expand = (iota((slots, edev), 0) // src_cap == iota((slots, edev), 1)).astype(F32).astype(BF16)
    slot_no = (iota((slots, tok), 0) % src_cap).astype(F32)
    for r in range(NREL):
        ahead = jnp.zeros_like(cnt[0])
        for q in range(NREL):
            if q != r:
                ahead = ahead + cnt[q] * (dev[q] < dev[r]).astype(F32)
        kept = jnp.where(pos[r] + ahead < cap, pos[r], -1.0).astype(BF16)
        dmat[r] = (jnp.dot(expand, kept, preferred_element_type=F32) == slot_no).astype(F32).astype(BF16)

    def gather_chunk(c):
        x_remote(c, 2).wait_recv()
        x_remote(c, 3).start()
        x_remote(c, 1).wait_recv()
        for r in range(NREL):
            if r == 3:
                x_remote(c, 3).wait_recv()
            part = jnp.dot(dmat[r], xall[r, c], preferred_element_type=F32).astype(BF16)
            xg[:, r] = part.reshape(edev, src_cap, ck)

    for c in range(NCH - 1):
        gather_chunk(c)

        def first_phase(j, carry):
            i0 = c * edev + j * PAIR
            for q in range(PAIR):
                w1_copy(i0 + q).wait()
            for q in range(PAIR):
                e = j * PAIR + q
                part = jnp.dot(xg[e].reshape(rows, ck), w1buf[(i0 + q) % NS1], preferred_element_type=F32)
                if c > 0:
                    part = hacc[e] + part
                hacc[e] = part
            for q in range(PAIR):
                w1_copy(i0 + q + NS1).start()
            return carry
        lax.fori_loop(0, edev // PAIR, first_phase, 0)

    last = (NCH - 1) * edev
    gather_chunk(NCH - 1)

    def second_phase(e, carry):
        w1_copy(last + e).wait()
        h = hacc[e] + jnp.dot(xg[e].reshape(rows, ck), w1buf[(last + e) % NS1], preferred_element_type=F32)

        @pl.when(e + NS1 < edev)
        def _():
            w1_copy(last + e + NS1).start()
        hb[...] = jax.nn.gelu(h, approximate=True).astype(BF16)
        w2_copy(e).wait()
        s = e % NS2
        b, q = e // eblk, e % eblk
        first = pl.multiple_of(q * src_cap, src_cap)
        for c in range(NCH):
            cols = pl.ds(c * ck, ck)
            z = jnp.dot(hb[...], w2buf[s, :, cols], preferred_element_type=F32).astype(BF16)
            zs[e, :, cols] = z
            zr[b, pl.ds(first, src_cap), cols] = z[:src_cap]

        @pl.when(e + NS2 < edev)
        def _():
            w2_copy(e + NS2).start()
        for r in (2, 3, 1):
            z_remote(e, r).start()
        return carry
    lax.fori_loop(0, edev, second_phase, 0)

    ncol = NREL * eblk * src_cap
    col = iota((1, ncol), 1)
    rel = col // (eblk * src_cap)
    rx, rc = rel // 2, rel % 2
    owner = 2 * (rx + mx - 2 * rx * mx) + (rc + mc - 2 * rc * mc)
    for b in range(nblk):
        for r in range(1, NREL):
            z_block(b, r).wait_recv()
        slot = ((owner * edev + b * eblk) * src_cap + col % (eblk * src_cap)).astype(F32)
        pick1 = (slot1 == slot).astype(F32).astype(BF16)
        pick2 = (slot2 == slot).astype(F32).astype(BF16)
        for c in range(NCH):
            cols = pl.ds(c * ck, ck)
            zc = zr[b, :, cols]
            mix = (gate1 * jnp.dot(pick1, zc, preferred_element_type=F32)
                   + gate2 * jnp.dot(pick2, zc, preferred_element_type=F32))
            if b > 0:
                mix = acc[:, cols] + mix
            if b < nblk - 1:
                acc[:, cols] = mix
            else:
                out_ref[:, cols] = (xall[0, c].astype(F32) + mix).astype(BF16)

    for r in range(1, NREL):
        s_remote(r).wait_send()
        for c in range(NCH):
            x_remote(c, r).wait_send()
        for b in range(nblk):
            z_block(b, r).wait_send()


def solution(mesh):
    group_size = mesh.shape['ep']
    row_spec = P(('dp', 'ep'), None)
    expert_spec = P('ep', None, None)

    def local_step(x_rows, logits, w_in, w_out):
        tok, d_model = x_rows.shape
        nexp = logits.shape[1]
        edev, _, ff = w_in.shape
        cap = 2 * tok * group_size // nexp
        src_cap = 4 * tok // nexp
        slots = edev * src_cap
        rows = NREL * src_cap
        ck = d_model // NCH
        eblk = 4
        nblk = edev // eblk
        dma = pltpu.SemaphoreType.DMA
        scratch = [
            pltpu.VMEM((NREL, NCH, tok, ck), BF16),
            pltpu.VMEM((nexp, tok), BF16),
            pltpu.VMEM((NREL, edev, tok), BF16),
            pltpu.VMEM((NREL, slots, tok), BF16),
            pltpu.VMEM((edev, NREL, src_cap, ck), BF16),
            pltpu.VMEM((edev, rows, ff), F32),
            pltpu.VMEM((rows, ff), BF16),
            pltpu.VMEM((NS1, ck, ff), BF16),
            pltpu.VMEM((NS2, ff, d_model), BF16),
            pltpu.VMEM((edev, rows, d_model), BF16),
            pltpu.VMEM((nblk, eblk * rows, d_model), BF16),
            pltpu.VMEM((tok, d_model), F32),
            dma((NS1,)), dma((NS2,)), dma((NCH,)),
            dma((NREL - 1, NCH)), dma((NREL - 1, NCH)),
            dma((NREL - 1,)), dma((NREL - 1,)),
            dma((NREL - 1, nblk)), dma((NREL - 1, nblk)),
        ]
        vmem = pl.BlockSpec(memory_space=pltpu.VMEM)
        hbm = pl.BlockSpec(memory_space=pl.ANY)
        return pl.pallas_call(
            functools.partial(moe_kernel, cap),
            out_shape=jax.ShapeDtypeStruct((tok, d_model), BF16),
            in_specs=[hbm, vmem, hbm, hbm],
            out_specs=vmem,
            scratch_shapes=scratch,
            compiler_params=pltpu.CompilerParams(collective_id=0, has_side_effects=True, vmem_limit_bytes=67000000),
        )(x_rows, logits, w_in, w_out)

    return jax.shard_map(local_step, mesh=mesh, in_specs=(row_spec, row_spec, expert_spec, expert_spec),
                         out_specs=row_spec, check_vma=False)
```

time: 247 us -> 88.5 us (0.36)
  waiting for transfers between devices: 89.2 us -> 0 us
  Pallas kernels: 0 us -> 84.4 us
  matrix products: 65.4 us -> 0 us
  local copies, waits for them, and re-layouts: 47.9 us -> 3.9 us
  other arithmetic: 24.2 us -> 0 us
  starting transfers between devices: 10.2 us -> 0 us
  blocking collectives: 8.6 us -> 0 us
    all_to_all x2 -> x0, waiting for transfers between devices: 89.2 us -> none  [the longest x1 47.1 us: local_step(): recv_buf = lax.all_to_all(send_buf, 'ep', 0, 0, tiled=True)]
    pallas_call x0 -> x1, Pallas kernels: none -> 84.4 us  [local_step(): pl.pallas_call(functools.partial(moe_kernel, cap), out_shape=jax.ShapeDty...]
    dot_general x2 -> x0, matrix products: 65.4 us -> none  [the longest x1 33.6 us: local_step(): jnp.einsum('ecd,edf->ecf', expert_rows, w_in, preferred_element_type=jnp....]
    gather x16 -> x0, local copies, waits for them, and re-layouts: 42.4 us -> none  [the longest x2 9.8 us: local_step(): rows_back = jnp.take(ret_buf, send_row, axis=0, mode='fill', fill_value=0)]
    all_to_all x2 -> x0, starting transfers between devices: 10.2 us -> none  [the longest x1 5.2 us: local_step(): ret_buf = lax.all_to_all(back_buf, 'ep', 0, 0, tiled=True)]
    reduce_sum x3 -> x0, other arithmetic: 10 us -> none  [the longest x1 9.9 us: local_step(): jnp.sum(pick_gate[:, :, None] * rows_back.astype(jnp.float32), axis=1)]
    select_n x9 -> x0, other arithmetic: 9.06 us -> none  [the longest x2 4.48 us: local_step(): jnp.take(expert_out, back_row.reshape(-1), axis=0, mode='fill', fill_valu...]
    unnamed x1 -> x0, blocking collectives: 8.6 us -> none
  transfers between devices with their start and end apart: 2 -> 0, of which waited for: 2 -> 0; matrix products, arithmetic and copies ran while one was open for 2% -> 0% of each run, Pallas kernels for 0% -> 0%
where the time goes in v1:
time: 88.5 us; the launch traced here: 88.3 us
  Pallas kernels  84.4 us (95%)
  local copies, waits for them, and re-layouts  3.9 us (4%)
    pallas_call x1, Pallas kernels, local_step(): pl.pallas_call(functools.partial(moe_kernel, cap), out_shape=jax.ShapeDty...  84.4 us
    unnamed x2, local copies, waits for them, and re-layouts  3.9 us

profile of v1, /device:TPU:0, one launch (start us, length us, event | category | flops | bytes accessed | tf_op | source)
XLA Modules:
  0.0 88.3 jit_solution(12137296175570009070)
XLA Ops:
  0.0 1.6 %copy.5.logits_ref = f32[256,64]{1,0:T(8,128)} copy(f32[256,64]{0,1:T(8,128)} %param.5) | data formatting | bytes 131072 | tf_op args[1]
  1.6 84.4 %shard_map.46 = bf16[256,2048]{1,0:T(8,128)(2,1)} custom-call(bf16[256,2048]{1,0:T(8,128)(2,1)} %x_hbm.1, f32[256,64]{1,0:T(8,128)} %copy.5.logits_ref, bf16[16,2048,1408]{2,1,0:T(8,128)(2,1)} %w1_hbm.1, bf16[16,1408,2048]{2,1,0:T(8,128)(2,1)} %w2_hbm.1), custom_call_target="tpu_custom_call" | custom-call | tf_op jit(solution)/shard_map/pallas_call | solution.py:266
  86.0 2.3 %copy.7 = bf16[256,2048]{1,0:T(8,128)(2,1)} copy(bf16[256,2048]{1,0:T(8,128)(2,1)} %shard_map.46) | data formatting | bytes 2097152

commit v2 on v1

v2 whole, which is shorter than its diff:
```python
import functools

import jax
import jax.numpy as jnp
from jax import lax
from jax.experimental import pallas as pl
from jax.experimental.pallas import tpu as pltpu
from jax.sharding import PartitionSpec as P

BF16 = jnp.bfloat16
F32 = jnp.float32
MESH = pl.DeviceIdType.MESH
NREL = 4
NCH = 4
NS1 = 12
NS2 = 3
PAIR = 2
UNIT = 16
PACKED = (1, 1, 1, 2, 1, 2, 2, 2)
FULL = (2, 2, 2, 2, 2, 2, 2, 2)


def iota(shape, dim):
    return lax.broadcasted_iota(jnp.int32, shape, dim)


def onehot(mask):
    return mask.astype(F32).astype(BF16)


def moe_kernel(cap, units, x_hbm, lt_ref, w1_hbm, w2_hbm, out_ref, flag_ref, xall, st_own, st_all, dmat, xg, hacc, hb,
               w1buf, w2buf, zs, pk, zr, acc, meta_own, meta_in, flag_own, flag_in, w1_sem, w2_sem, xl_sem, xs_sem,
               xr_sem, ss_sem, sr_sem, ms_sem, mr_sem, fs_sem, fr_sem, ps_sem, pr_sem, zs_sem, zr_sem):
    nexp, tok = lt_ref.shape
    edev, d_model, ff = w1_hbm.shape
    src_cap = xg.shape[2]
    slots = edev * src_cap
    ck = d_model // NCH
    rows = NREL * src_cap
    nblk = edev // PAIR
    starts = [sum(units[:b]) for b in range(nblk + 1)]
    total_rows = starts[nblk] * UNIT
    split_blk = nblk - 2
    split = starts[split_blk] * UNIT

    me = lax.axis_index('ep')
    group = lax.axis_index('dp')
    ngroups = lax.axis_size('dp')
    mx, mc = me // 2, me % 2
    dev = [me, 2 * mx + (1 - mc), 2 * (1 - mx) + mc, 2 * (1 - mx) + (1 - mc)]

    def remote(src, dst, send, recv, r):
        return pltpu.make_async_remote_copy(src_ref=src, dst_ref=dst, send_sem=send, recv_sem=recv,
                                            device_id={'ep': dev[r]}, device_id_type=MESH)

    def w1_copy(i):
        c, e = i // edev, i % edev
        k = pl.multiple_of(c * ck, ck)
        s = i % NS1
        return pltpu.make_async_copy(w1_hbm.at[e, pl.ds(k, ck), :], w1buf.at[s], w1_sem.at[s])

    def w2_copy(e):
        s = e % NS2
        return pltpu.make_async_copy(w2_hbm.at[e], w2buf.at[s], w2_sem.at[s])

    def x_local(c):
        return pltpu.make_async_copy(x_hbm.at[:, pl.ds(c * ck, ck)], xall.at[0, c], xl_sem.at[c])

    def x_remote(c, slot):
        return remote(xall.at[2 if slot == 3 else 0, c], xall.at[slot, c], xs_sem.at[slot - 1, c],
                      xr_sem.at[slot - 1, c], 2 if slot == 2 else 1)

    def s_remote(r):
        first = pl.multiple_of(dev[r] * edev, edev)
        return remote(st_own.at[pl.ds(first, edev), :], st_all.at[r], ss_sem.at[r - 1], sr_sem.at[r - 1], r)

    def m_remote(r):
        return remote(meta_own.at[r], meta_in.at[r], ms_sem.at[r - 1], mr_sem.at[r - 1], r)

    def f_remote(k):
        peer = lax.rem(group + k, ngroups)
        return pltpu.make_async_remote_copy(src_ref=flag_own, dst_ref=flag_in.at[k], send_sem=fs_sem.at[k - 1],
                                            recv_sem=fr_sem.at[k - 1], device_id={'dp': peer}, device_id_type=MESH)

    def partner_remote(e):
        first = pl.multiple_of(e * src_cap, src_cap)
        return remote(zs.at[1, pl.ds(first, src_cap), :], zr.at[1, pl.ds(first, src_cap), :], ps_sem.at[0],
                      pr_sem.at[0], 1)

    def partner_all():
        return remote(zr.at[1], zr.at[1], ps_sem.at[0], pr_sem.at[0], 1)

    def pack_remote(r, first, part):
        return remote(pk.at[r - 2, pl.ds(first, UNIT), :], zr.at[r, pl.ds(first, UNIT), :], zs_sem.at[r - 2, part],
                      zr_sem.at[r - 2, part], r)

    def pack_part(r, part):
        span = pl.ds(0, split) if part == 0 else pl.ds(split, total_rows - split)
        ref = zr.at[r, span, :]
        return remote(ref, ref, zs_sem.at[r - 2, part], zr_sem.at[r - 2, part], r)

    barrier = pltpu.get_barrier_semaphore()
    for r in range(1, NREL):
        pl.semaphore_signal(barrier, inc=1, device_id={'ep': dev[r]}, device_id_type=MESH)
    for k in range(1, ngroups):
        pl.semaphore_signal(barrier, inc=1, device_id={'dp': lax.rem(group + k, ngroups)}, device_id_type=MESH)
    for c in range(NCH):
        x_local(c).start()

    def start_w1(i, carry):
        w1_copy(i).start()
        return carry
    lax.fori_loop(0, NS1, start_w1, 0)
    for e in range(NS2):
        w2_copy(e).start()

    for r in (2, 3):
        zs[r] = jnp.zeros(zs.shape[1:], BF16)
    meta_own[...] = jnp.zeros_like(meta_own)
    pl.semaphore_wait(barrier, NREL - 1 + ngroups - 1)
    x_local(0).wait()
    x_remote(0, 2).start()
    x_remote(0, 1).start()

    lt = lt_ref[...]
    m1t = jnp.max(lt, axis=0, keepdims=True)
    m2t = jnp.max(jnp.where(lt == m1t, -jnp.inf, lt), axis=0, keepdims=True)
    chosen_t = lt >= m2t
    upper = onehot(iota((tok, tok), 0) < iota((tok, tok), 1))
    before_t = jnp.dot(onehot(chosen_t), upper, preferred_element_type=F32)
    st_own[...] = jnp.where(chosen_t, before_t, -1.0).astype(BF16)

    logits = lt.T
    m1 = jnp.max(logits, axis=1, keepdims=True)
    is1 = logits == m1
    rest = jnp.where(is1, -jnp.inf, logits)
    m2 = jnp.max(rest, axis=1, keepdims=True)
    is2 = rest == m2
    lower = onehot(iota((tok, tok), 1) < iota((tok, tok), 0))
    before = jnp.dot(lower, onehot(jnp.logical_or(is1, is2)), preferred_element_type=F32)
    total = jnp.sum(jnp.exp(logits - m1), axis=1, keepdims=True)
    gate1 = 1.0 / total
    gate2 = jnp.exp(m2 - m1) / total

    for r in (2, 3, 1):
        s_remote(r).start()
    for c in range(1, NCH):
        x_local(c).wait()
        x_remote(c, 2).start()
        x_remote(c, 1).start()

    for r in range(1, NREL):
        s_remote(r).wait_recv()
    own_first = pl.multiple_of(me * edev, edev)
    pos = [st_own[pl.ds(own_first, edev), :].astype(F32)] + [st_all[r].astype(F32) for r in range(1, NREL)]
    cnt = [jnp.sum((p >= 0.0).astype(F32), axis=1, keepdims=True) for p in pos]
    ahead = []
    for r in range(NREL):
        a = jnp.zeros_like(cnt[0])
        for q in range(NREL):
            if q != r:
                a = a + cnt[q] * (dev[q] < dev[r]).astype(F32)
        ahead.append(a)

    lane_exp = iota((edev, 128), 1) - me * edev == iota((edev, 128), 0)
    exp_no = iota((edev, 1), 0)
    exp_row = exp_no.astype(F32)
    wide = iota((edev, slots), 1)
    own_slot = wide // src_cap == iota((edev, slots), 0)
    over = jnp.zeros((1, 1), F32)
    packed_row = [None, None]
    own_meta = None
    for r in range(NREL):
        if r < 2:
            base = exp_row * src_cap
            rows_kept = jnp.full((edev, 1), float(src_cap), F32)
        else:
            rows_kept = jnp.clip(cap - ahead[r], 0.0, cnt[r])
            base = jnp.zeros((edev, 1), F32)
            end = jnp.zeros((1, 1), F32)
            for b in range(nblk):
                end = jnp.maximum(end, float(starts[b] * UNIT))
                for q in range(PAIR):
                    e = b * PAIR + q
                    base = jnp.where(exp_no == e, end, base)
                    end = end + rows_kept[e:e + 1]
            over = jnp.maximum(over, (end > float(total_rows)).astype(F32))
            row = jnp.where(own_slot, base + (wide % src_cap).astype(F32), 0.0)
            row = jnp.where((wide % src_cap).astype(F32) < rows_kept, row, jnp.where(own_slot, -1.0, 0.0))
            packed_row[r - 2] = jnp.sum(row, axis=0, keepdims=True)
        base_lane = jnp.sum(jnp.where(lane_exp, base + float(r * slots), 0.0), axis=0, keepdims=True)
        kept_lane = jnp.sum(jnp.where(lane_exp, rows_kept, 0.0), axis=0, keepdims=True)
        if r == 0:
            own_meta = (base_lane, kept_lane)
        else:
            meta_own[r, 0:1, :] = base_lane
            meta_own[r, 1:2, :] = kept_lane
    for r in range(1, NREL):
        meta_own[r, 2:3, :] = jnp.broadcast_to(over, (1, 128))

    expand = onehot(iota((slots, edev), 0) // src_cap == iota((slots, edev), 1))
    slot_no = (iota((slots, tok), 0) % src_cap).astype(F32)
    for r in range(NREL):
        kept = jnp.where(pos[r] + ahead[r] < cap, pos[r], -1.0).astype(BF16)
        dmat[r] = onehot(jnp.dot(expand, kept, preferred_element_type=F32) == slot_no)
    for r in (2, 3, 1):
        m_remote(r).start()

    def gather_chunk(c):
        x_remote(c, 2).wait_recv()
        x_remote(c, 3).start()
        x_remote(c, 1).wait_recv()
        for r in range(NREL):
            if r == 3:
                x_remote(c, 3).wait_recv()
            part = jnp.dot(dmat[r], xall[r, c], preferred_element_type=F32).astype(BF16)
            xg[:, r] = part.reshape(edev, src_cap, ck)

    for c in range(NCH - 1):
        gather_chunk(c)

        def first_phase(j, carry):
            i0 = c * edev + j * PAIR
            for q in range(PAIR):
                w1_copy(i0 + q).wait()
            for q in range(PAIR):
                e = j * PAIR + q
                part = jnp.dot(xg[e].reshape(rows, ck), w1buf[(i0 + q) % NS1], preferred_element_type=F32)
                if c > 0:
                    part = hacc[e] + part
                hacc[e] = part
            for q in range(PAIR):
                w1_copy(i0 + q + NS1).start()
            return carry
        lax.fori_loop(0, edev // PAIR, first_phase, 0)

        if c == 0:
            for r in range(1, NREL):
                m_remote(r).wait_recv()
            first_row, kept_rows = own_meta
            for r in range(1, NREL):
                first_row = first_row + meta_in[r, 0:1, :]
                kept_rows = kept_rows + meta_in[r, 1:2, :]
                over = jnp.maximum(over, meta_in[r, 2:3, 0:1])
            flag_own[...] = jnp.broadcast_to(over, flag_own.shape)
            place = jnp.where(before < kept_rows[:, :nexp], first_row[:, :nexp] + before, -1.0)
            slot1 = jnp.sum(jnp.where(is1, place, 0.0), axis=1, keepdims=True)
            slot2 = jnp.sum(jnp.where(is2, place, 0.0), axis=1, keepdims=True)
        if c == 1:
            for k in range(1, ngroups):
                f_remote(k).start()

    last = (NCH - 1) * edev
    gather_chunk(NCH - 1)

    def block(b, carry):
        for q in range(PAIR):
            e = b * PAIR + q
            w1_copy(last + e).wait()
            h = hacc[e] + jnp.dot(xg[e].reshape(rows, ck), w1buf[(last + e) % NS1], preferred_element_type=F32)

            @pl.when(e + NS1 < edev)
            def _():
                w1_copy(last + e + NS1).start()
            hb[...] = jax.nn.gelu(h, approximate=True).astype(BF16)
            w2_copy(e).wait()
            first = pl.multiple_of(e * src_cap, src_cap)
            for c in range(NCH):
                cols = pl.ds(c * ck, ck)
                z = jnp.dot(hb[...], w2buf[e % NS2, :, cols], preferred_element_type=F32).astype(BF16)
                zr[0, pl.ds(first, src_cap), cols] = z[:src_cap]
                for r in range(1, NREL):
                    zs[r, pl.ds(first, src_cap), cols] = z[r * src_cap:(r + 1) * src_cap]

            @pl.when(e + NS2 < edev)
            def _():
                w2_copy(e + NS2).start()
            partner_remote(e).start()
        start = sum((b > j).astype(jnp.int32) * units[j] for j in range(nblk - 1)) * UNIT
        start = pl.multiple_of(start, UNIT)
        double = functools.reduce(jnp.logical_or, [b == j for j in range(nblk) if units[j] == 2])
        part = (b >= split_blk).astype(jnp.int32)
        for r in (2, 3):
            row = (iota((2 * UNIT, slots), 0) + start).astype(F32)
            pick = onehot(row == packed_row[r - 2])
            for c in range(NCH):
                cols = pl.ds(c * ck, ck)
                pk[r - 2, pl.ds(start, 2 * UNIT), cols] = jnp.dot(pick, zs[r, :, cols],
                                                                  preferred_element_type=F32).astype(BF16)
        for r in (2, 3):
            pack_remote(r, start, part).start()

            @pl.when(double)
            def _():
                pack_remote(r, start + UNIT, part).start()
        return carry
    lax.fori_loop(0, nblk, block, 0)

    for k in range(1, ngroups):
        f_remote(k).wait_recv()
    flag = flag_own[...]
    for k in range(1, ngroups):
        flag = jnp.maximum(flag, flag_in[k])
    flag_ref[...] = flag

    pieces = [(0, 0, slots, None), (1, 0, slots, 'partner'), (2, 0, split, 0), (3, 0, split, 0),
              (2, split, total_rows - split, 1), (3, split, total_rows - split, 1)]
    for n, (r, first, size, wait) in enumerate(pieces):
        if wait == 'partner':
            partner_all().wait_recv()
        elif wait is not None:
            pack_part(r, wait).wait_recv()
        slot = (iota((1, size), 1) + (r * slots + first)).astype(F32)
        pick1 = onehot(slot1 == slot)
        pick2 = onehot(slot2 == slot)
        for c in range(NCH):
            cols = pl.ds(c * ck, ck)
            zc = zr[r, first:first + size, cols]
            mix = (gate1 * jnp.dot(pick1, zc, preferred_element_type=F32)
                   + gate2 * jnp.dot(pick2, zc, preferred_element_type=F32))
            if n > 0:
                mix = acc[:, cols] + mix
            if n < len(pieces) - 1:
                acc[:, cols] = mix
            else:
                out_ref[:, cols] = (xall[0, c].astype(F32) + mix).astype(BF16)

    for k in range(1, ngroups):
        f_remote(k).wait_send()
    partner_all().wait_send()
    for r in range(1, NREL):
        s_remote(r).wait_send()
        m_remote(r).wait_send()
        for c in range(NCH):
            x_remote(c, r).wait_send()
        if r >= 2:
            for part in range(2):
                pack_part(r, part).wait_send()


def solution(mesh):
    group_size = mesh.shape['ep']
    ngroups = mesh.shape['dp']
    row_spec = P(('dp', 'ep'), None)
    expert_spec = P('ep', None, None)

    def call(units, collective, x_rows, logits_t, w_in, w_out):
        tok, d_model = x_rows.shape
        nexp = logits_t.shape[0]
        edev, _, ff = w_in.shape
        cap = 2 * tok * group_size // nexp
        src_cap = 4 * tok // nexp
        slots = edev * src_cap
        rows = NREL * src_cap
        ck = d_model // NCH
        dma = pltpu.SemaphoreType.DMA
        scratch = [
            pltpu.VMEM((NREL, NCH, tok, ck), BF16),
            pltpu.VMEM((nexp, tok), BF16),
            pltpu.VMEM((NREL, edev, tok), BF16),
            pltpu.VMEM((NREL, slots, tok), BF16),
            pltpu.VMEM((edev, NREL, src_cap, ck), BF16),
            pltpu.VMEM((edev, rows, ff), F32),
            pltpu.VMEM((rows, ff), BF16),
            pltpu.VMEM((NS1, ck, ff), BF16),
            pltpu.VMEM((NS2, ff, d_model), BF16),
            pltpu.VMEM((NREL, slots, d_model), BF16),
            pltpu.VMEM((2, sum(units) * UNIT, d_model), BF16),
            pltpu.VMEM((NREL, slots, d_model), BF16),
            pltpu.VMEM((tok, d_model), F32),
            pltpu.VMEM((NREL, 8, 128), F32), pltpu.VMEM((NREL, 8, 128), F32),
            pltpu.VMEM((8, 128), F32), pltpu.VMEM((ngroups, 8, 128), F32),
            dma((NS1,)), dma((NS2,)), dma((NCH,)),
            dma((NREL - 1, NCH)), dma((NREL - 1, NCH)),
            dma((NREL - 1,)), dma((NREL - 1,)),
            dma((NREL - 1,)), dma((NREL - 1,)),
            dma((ngroups - 1,)), dma((ngroups - 1,)),
            dma((1,)), dma((1,)),
            dma((2, 2)), dma((2, 2)),
        ]
        vmem = pl.BlockSpec(memory_space=pltpu.VMEM)
        hbm = pl.BlockSpec(memory_space=pl.ANY)
        return pl.pallas_call(
            functools.partial(moe_kernel, cap, units),
            out_shape=(jax.ShapeDtypeStruct((tok, d_model), BF16), jax.ShapeDtypeStruct((8, 128), F32)),
            in_specs=[hbm, vmem, hbm, hbm],
            out_specs=(vmem, vmem),
            scratch_shapes=scratch,
            compiler_params=pltpu.CompilerParams(collective_id=collective, has_side_effects=True,
                                                 vmem_limit_bytes=67000000),
        )(x_rows, logits_t, w_in, w_out)

    def local_step(x_rows, logits, w_in, w_out):
        args = (x_rows, logits.T, w_in, w_out)
        out, flag = call(PACKED, 0, *args)
        return lax.cond(flag[0, 0] > 0.0, lambda: call(FULL, 1, *args)[0], lambda: out)

    return jax.shard_map(local_step, mesh=mesh, in_specs=(row_spec, row_spec, expert_spec, expert_spec),
                         out_specs=row_spec, check_vma=False)
```

time: 88.5 us -> 92.5 us (1.045)
  Pallas kernels: 84.4 us -> 88 us
    pallas_call x1, Pallas kernels: 84.4 us -> 88 us  [call(): pl.pallas_call(functools.partial(moe_kernel, cap, units), out_shape=(jax....]
    unnamed x2 -> x1, local copies, waits for them, and re-layouts: 3.9 us -> 2.3 us
    slice x0 -> x1, local copies, waits for them, and re-layouts: none -> 1.19 us  [local_step(): flag[0, 0] > 0.0]
where the time goes in v2:
time: 92.5 us; the launch traced here: 92.3 us
  Pallas kernels  88 us (95%)
  local copies, waits for them, and re-layouts  3.49 us (4%)
    pallas_call x1, Pallas kernels, call(): pl.pallas_call(functools.partial(moe_kernel, cap, units), out_shape=(jax....  88 us
    unnamed x1, local copies, waits for them, and re-layouts  2.3 us

profile of v2, /device:TPU:0, one launch (start us, length us, event | category | flops | bytes accessed | tf_op | source)
XLA Modules:
  0.0 92.3 jit_solution(2588132728407162878)
XLA Ops:
  0.0 88.0 %shard_map.48 = (bf16[256,2048]{1,0:T(8,128)(2,1)}, f32[8,128]{1,0:T(8,128)}) custom-call(bf16[256,2048]{1,0:T(8,128)(2,1)} %x_hbm.1, f32[64,256]{1,0:T(8,128)} %bitcast.2, bf16[16,2048,1408]{2,1,0:T(8,128)(2,1)} %w1_hbm.1, bf16[16,1408,2048]{2,1,0:T(8,128)(2,1)} %w2_hbm.1), custom_call_target="tpu_custom_call" | custom-call | tf_op jit(solution)/shard_map/pallas_call | solution.py:383
  88.0 1.2 %slice.3 = f32[1,1]{1,0:T(1,128)} slice(f32[8,128]{1,0:T(8,128)} %get-tuple-element.24), slice={[0:1], [0:1]} | slice | bytes 8 | tf_op jit(solution)/shard_map/slice | solution.py:396
  89.8 0.2 conditional.1
  90.0 2.3 %copy.10 = bf16[256,2048]{1,0:T(8,128)(2,1)} copy(bf16[256,2048]{1,0:T(8,128)(2,1)} %get-tuple-element.26) | data formatting | bytes 2097152

commit v3 on v2

--- a/solution.py
+++ b/solution.py
@@ -12,12 +12,13 @@
 MESH = pl.DeviceIdType.MESH
 NREL = 4
 NCH = 4
-NS1 = 12
+NS1 = 14
 NS2 = 3
-PAIR = 2
+STEP = 4
 UNIT = 16
-PACKED = (1, 1, 1, 2, 1, 2, 2, 2)
-FULL = (2, 2, 2, 2, 2, 2, 2, 2)
+TAIL = 2
+PACKED = (0, 1, 1, 0, 1, 0, 1, 0, 1, 1, 1, 1, 1, 1, 1, 1)
+FULL = (1,) * 16
 
 
 def iota(shape, dim):
@@ -29,7 +30,7 @@
 
 
 def moe_kernel(cap, units, x_hbm, lt_ref, w1_hbm, w2_hbm, out_ref, flag_ref, xall, st_own, st_all, dmat, xg, hacc, hb,
-               w1buf, w2buf, zs, pk, zr, acc, meta_own, meta_in, flag_own, flag_in, w1_sem, w2_sem, xl_sem, xs_sem,
+               w1buf, w2buf, zs, pk, zr, meta_own, meta_in, flag_own, flag_in, choice, w1_sem, w2_sem, xl_sem, xs_sem,
                xr_sem, ss_sem, sr_sem, ms_sem, mr_sem, fs_sem, fr_sem, ps_sem, pr_sem, zs_sem, zr_sem):
     nexp, tok = lt_ref.shape
     edev, d_model, ff = w1_hbm.shape
@@ -37,11 +38,8 @@
     slots = edev * src_cap
     ck = d_model // NCH
     rows = NREL * src_cap
-    nblk = edev // PAIR
-    starts = [sum(units[:b]) for b in range(nblk + 1)]
-    total_rows = starts[nblk] * UNIT
-    split_blk = nblk - 2
-    split = starts[split_blk] * UNIT
+    total_rows = sum(units) * UNIT
+    split = total_rows - TAIL * UNIT
 
     me = lax.axis_index('ep')
     group = lax.axis_index('dp')
@@ -84,7 +82,7 @@
 
     def partner_remote(e):
         first = pl.multiple_of(e * src_cap, src_cap)
-        return remote(zs.at[1, pl.ds(first, src_cap), :], zr.at[1, pl.ds(first, src_cap), :], ps_sem.at[0],
+        return remote(zs.at[0, pl.ds(first, src_cap), :], zr.at[1, pl.ds(first, src_cap), :], ps_sem.at[0],
                       pr_sem.at[0], 1)
 
     def partner_all():
@@ -115,12 +113,8 @@
         w2_copy(e).start()
 
     for r in (2, 3):
-        zs[r] = jnp.zeros(zs.shape[1:], BF16)
+        zs[r - 1] = jnp.zeros(zs.shape[1:], BF16)
     meta_own[...] = jnp.zeros_like(meta_own)
-    pl.semaphore_wait(barrier, NREL - 1 + ngroups - 1)
-    x_local(0).wait()
-    x_remote(0, 2).start()
-    x_remote(0, 1).start()
 
     lt = lt_ref[...]
     m1t = jnp.max(lt, axis=0, keepdims=True)
@@ -129,6 +123,14 @@
     upper = onehot(iota((tok, tok), 0) < iota((tok, tok), 1))
     before_t = jnp.dot(onehot(chosen_t), upper, preferred_element_type=F32)
     st_own[...] = jnp.where(chosen_t, before_t, -1.0).astype(BF16)
+
+    pl.semaphore_wait(barrier, NREL - 1 + ngroups - 1)
+    for r in (2, 3, 1):
+        s_remote(r).start()
+    for c in range(NCH):
+        x_local(c).wait()
+        x_remote(c, 2).start()
+        x_remote(c, 1).start()
 
     logits = lt.T
     m1 = jnp.max(logits, axis=1, keepdims=True)
@@ -141,13 +143,6 @@
     total = jnp.sum(jnp.exp(logits - m1), axis=1, keepdims=True)
     gate1 = 1.0 / total
     gate2 = jnp.exp(m2 - m1) / total
-
-    for r in (2, 3, 1):
-        s_remote(r).start()
-    for c in range(1, NCH):
-        x_local(c).wait()
-        x_remote(c, 2).start()
-        x_remote(c, 1).start()
 
     for r in range(1, NREL):
         s_remote(r).wait_recv()
@@ -178,12 +173,10 @@
             rows_kept = jnp.clip(cap - ahead[r], 0.0, cnt[r])
             base = jnp.zeros((edev, 1), F32)
             end = jnp.zeros((1, 1), F32)
-            for b in range(nblk):
-                end = jnp.maximum(end, float(starts[b] * UNIT))
-                for q in range(PAIR):
-                    e = b * PAIR + q
-                    base = jnp.where(exp_no == e, end, base)
-                    end = end + rows_kept[e:e + 1]
+            for e in range(edev):
+                end = jnp.maximum(end, float(sum(units[:e]) * UNIT))
+                base = jnp.where(exp_no == e, end, base)
+                end = end + rows_kept[e:e + 1]
             over = jnp.maximum(over, (end > float(total_rows)).astype(F32))
             row = jnp.where(own_slot, base + (wide % src_cap).astype(F32), 0.0)
             row = jnp.where((wide % src_cap).astype(F32) < rows_kept, row, jnp.where(own_slot, -1.0, 0.0))
@@ -220,81 +213,82 @@
         gather_chunk(c)
 
         def first_phase(j, carry):
-            i0 = c * edev + j * PAIR
-            for q in range(PAIR):
+            i0 = c * edev + j * STEP
+            for q in range(STEP):
                 w1_copy(i0 + q).wait()
-            for q in range(PAIR):
-                e = j * PAIR + q
+            for q in range(STEP):
+                e = j * STEP + q
                 part = jnp.dot(xg[e].reshape(rows, ck), w1buf[(i0 + q) % NS1], preferred_element_type=F32)
                 if c > 0:
                     part = hacc[e] + part
                 hacc[e] = part
-            for q in range(PAIR):
+            for q in range(STEP):
                 w1_copy(i0 + q + NS1).start()
             return carry
-        lax.fori_loop(0, edev // PAIR, first_phase, 0)
-
-        if c == 0:
-            for r in range(1, NREL):
-                m_remote(r).wait_recv()
-            first_row, kept_rows = own_meta
-            for r in range(1, NREL):
-                first_row = first_row + meta_in[r, 0:1, :]
-                kept_rows = kept_rows + meta_in[r, 1:2, :]
-                over = jnp.maximum(over, meta_in[r, 2:3, 0:1])
-            flag_own[...] = jnp.broadcast_to(over, flag_own.shape)
-            place = jnp.where(before < kept_rows[:, :nexp], first_row[:, :nexp] + before, -1.0)
-            slot1 = jnp.sum(jnp.where(is1, place, 0.0), axis=1, keepdims=True)
-            slot2 = jnp.sum(jnp.where(is2, place, 0.0), axis=1, keepdims=True)
-        if c == 1:
+        lax.fori_loop(0, edev // STEP, first_phase, 0)
+
+    last = (NCH - 1) * edev
+    gather_chunk(NCH - 1)
+
+    def place_rows():
+        for r in range(1, NREL):
+            m_remote(r).wait_recv()
+        first_row, kept_rows = own_meta
+        flag = over
+        for r in range(1, NREL):
+            first_row = first_row + meta_in[r, 0:1, :]
+            kept_rows = kept_rows + meta_in[r, 1:2, :]
+            flag = jnp.maximum(flag, meta_in[r, 2:3, 0:1])
+        flag_own[...] = jnp.broadcast_to(flag, flag_own.shape)
+        place = jnp.where(before < kept_rows[:, :nexp], first_row[:, :nexp] + before, -1.0)
+        choice[:, 0:1] = jnp.sum(jnp.where(is1, place, 0.0), axis=1, keepdims=True)
+        choice[:, 1:2] = jnp.sum(jnp.where(is2, place, 0.0), axis=1, keepdims=True)
+
+    def second_phase(e, carry):
+        @pl.when(e == edev // 4)
+        def _():
+            place_rows()
+
+        @pl.when(e == edev // 2)
+        def _():
             for k in range(1, ngroups):
                 f_remote(k).start()
-
-    last = (NCH - 1) * edev
-    gather_chunk(NCH - 1)
-
-    def block(b, carry):
-        for q in range(PAIR):
-            e = b * PAIR + q
-            w1_copy(last + e).wait()
-            h = hacc[e] + jnp.dot(xg[e].reshape(rows, ck), w1buf[(last + e) % NS1], preferred_element_type=F32)
-
-            @pl.when(e + NS1 < edev)
-            def _():
-                w1_copy(last + e + NS1).start()
-            hb[...] = jax.nn.gelu(h, approximate=True).astype(BF16)
-            w2_copy(e).wait()
-            first = pl.multiple_of(e * src_cap, src_cap)
-            for c in range(NCH):
-                cols = pl.ds(c * ck, ck)
-                z = jnp.dot(hb[...], w2buf[e % NS2, :, cols], preferred_element_type=F32).astype(BF16)
-                zr[0, pl.ds(first, src_cap), cols] = z[:src_cap]
-                for r in range(1, NREL):
-                    zs[r, pl.ds(first, src_cap), cols] = z[r * src_cap:(r + 1) * src_cap]
-
-            @pl.when(e + NS2 < edev)
-            def _():
-                w2_copy(e + NS2).start()
-            partner_remote(e).start()
-        start = sum((b > j).astype(jnp.int32) * units[j] for j in range(nblk - 1)) * UNIT
-        start = pl.multiple_of(start, UNIT)
-        double = functools.reduce(jnp.logical_or, [b == j for j in range(nblk) if units[j] == 2])
-        part = (b >= split_blk).astype(jnp.int32)
-        for r in (2, 3):
-            row = (iota((2 * UNIT, slots), 0) + start).astype(F32)
-            pick = onehot(row == packed_row[r - 2])
-            for c in range(NCH):
-                cols = pl.ds(c * ck, ck)
-                pk[r - 2, pl.ds(start, 2 * UNIT), cols] = jnp.dot(pick, zs[r, :, cols],
+        w1_copy(last + e).wait()
+        h = hacc[e] + jnp.dot(xg[e].reshape(rows, ck), w1buf[(last + e) % NS1], preferred_element_type=F32)
+
+        @pl.when(e + NS1 < edev)
+        def _():
+            w1_copy(last + e + NS1).start()
+        hb[...] = jax.nn.gelu(h, approximate=True).astype(BF16)
+        w2_copy(e).wait()
+        first = pl.multiple_of(e * src_cap, src_cap)
+        for c in range(NCH):
+            cols = pl.ds(c * ck, ck)
+            z = jnp.dot(hb[...], w2buf[e % NS2, :, cols], preferred_element_type=F32).astype(BF16)
+            zr[0, pl.ds(first, src_cap), cols] = z[:src_cap]
+            for r in range(1, NREL):
+                zs[r - 1, pl.ds(first, src_cap), cols] = z[r * src_cap:(r + 1) * src_cap]
+
+        @pl.when(e + NS2 < edev)
+        def _():
+            w2_copy(e + NS2).start()
+
+        @pl.when(functools.reduce(jnp.logical_or, [e == j for j in range(edev) if units[j]]))
+        def _():
+            start = sum((e > j).astype(jnp.int32) for j in range(edev - 1) if units[j]) * UNIT
+            start = pl.multiple_of(start, UNIT)
+            for r in (2, 3):
+                row = (iota((UNIT, slots), 0) + start).astype(F32)
+                pick = onehot(row == packed_row[r - 2])
+                for c in range(NCH):
+                    cols = pl.ds(c * ck, ck)
+                    pk[r - 2, pl.ds(start, UNIT), cols] = jnp.dot(pick, zs[r - 1, :, cols],
                                                                   preferred_element_type=F32).astype(BF16)
-        for r in (2, 3):
-            pack_remote(r, start, part).start()
-
-            @pl.when(double)
-            def _():
-                pack_remote(r, start + UNIT, part).start()
+            for r in (2, 3):
+                pack_remote(r, start, (start >= split).astype(jnp.int32)).start()
+        partner_remote(e).start()
         return carry
-    lax.fori_loop(0, nblk, block, 0)
+    lax.fori_loop(0, edev, second_phase, 0)
 
     for k in range(1, ngroups):
         f_remote(k).wait_recv()
@@ -303,27 +297,26 @@
         flag = jnp.maximum(flag, flag_in[k])
     flag_ref[...] = flag
 
-    pieces = [(0, 0, slots, None), (1, 0, slots, 'partner'), (2, 0, split, 0), (3, 0, split, 0),
-              (2, split, total_rows - split, 1), (3, split, total_rows - split, 1)]
-    for n, (r, first, size, wait) in enumerate(pieces):
-        if wait == 'partner':
-            partner_all().wait_recv()
-        elif wait is not None:
-            pack_part(r, wait).wait_recv()
-        slot = (iota((1, size), 1) + (r * slots + first)).astype(F32)
+    slot1, slot2 = choice[:, 0:1], choice[:, 1:2]
+    far = total_rows - split
+    pieces = [((0,), 0, slots), ((1,), 0, slots), ((2, 3), 0, split), ((2, 3), split, far)]
+    for n, (rels, first, size) in enumerate(pieces):
+        for r in rels:
+            if r == 1:
+                partner_all().wait_recv()
+            elif r >= 2:
+                pack_part(r, n - 2).wait_recv()
+        slot = jnp.concatenate([(iota((1, size), 1) + (r * slots + first)).astype(F32) for r in rels], axis=1)
         pick1 = onehot(slot1 == slot)
         pick2 = onehot(slot2 == slot)
         for c in range(NCH):
             cols = pl.ds(c * ck, ck)
-            zc = zr[r, first:first + size, cols]
+            zc = jnp.concatenate([zr[r, first:first + size, cols] for r in rels], axis=0)
             mix = (gate1 * jnp.dot(pick1, zc, preferred_element_type=F32)
                    + gate2 * jnp.dot(pick2, zc, preferred_element_type=F32))
             if n > 0:
-                mix = acc[:, cols] + mix
-            if n < len(pieces) - 1:
-                acc[:, cols] = mix
-            else:
-                out_ref[:, cols] = (xall[0, c].astype(F32) + mix).astype(BF16)
+                mix = out_ref[:, cols] + mix
+            out_ref[:, cols] = mix
 
     for k in range(1, ngroups):
         f_remote(k).wait_send()
@@ -364,12 +357,11 @@
             pltpu.VMEM((rows, ff), BF16),
             pltpu.VMEM((NS1, ck, ff), BF16),
             pltpu.VMEM((NS2, ff, d_model), BF16),
-            pltpu.VMEM((NREL, slots, d_model), BF16),
+            pltpu.VMEM((NREL - 1, slots, d_model), BF16),
             pltpu.VMEM((2, sum(units) * UNIT, d_model), BF16),
             pltpu.VMEM((NREL, slots, d_model), BF16),
-            pltpu.VMEM((tok, d_model), F32),
             pltpu.VMEM((NREL, 8, 128), F32), pltpu.VMEM((NREL, 8, 128), F32),
-            pltpu.VMEM((8, 128), F32), pltpu.VMEM((ngroups, 8, 128), F32),
+            pltpu.VMEM((8, 128), F32), pltpu.VMEM((ngroups, 8, 128), F32), pltpu.VMEM((tok, 128), F32),
             dma((NS1,)), dma((NS2,)), dma((NCH,)),
             dma((NREL - 1, NCH)), dma((NREL - 1, NCH)),
             dma((NREL - 1,)), dma((NREL - 1,)),
@@ -382,7 +374,7 @@
         hbm = pl.BlockSpec(memory_space=pl.ANY)
         return pl.pallas_call(
             functools.partial(moe_kernel, cap, units),
-            out_shape=(jax.ShapeDtypeStruct((tok, d_model), BF16), jax.ShapeDtypeStruct((8, 128), F32)),
+            out_shape=(jax.ShapeDtypeStruct((tok, d_model), F32), jax.ShapeDtypeStruct((8, 128), F32)),
             in_specs=[hbm, vmem, hbm, hbm],
             out_specs=(vmem, vmem),
             scratch_shapes=scratch,
@@ -392,8 +384,9 @@
 
     def local_step(x_rows, logits, w_in, w_out):
         args = (x_rows, logits.T, w_in, w_out)
-        out, flag = call(PACKED, 0, *args)
-        return lax.cond(flag[0, 0] > 0.0, lambda: call(FULL, 1, *args)[0], lambda: out)
+        mix, flag = call(PACKED, 0, *args)
+        mix = lax.cond(flag[0, 0] > 0.0, lambda: call(FULL, 1, *args)[0], lambda: mix)
+        return (x_rows.astype(F32) + mix).astype(BF16)
 
     return jax.shard_map(local_step, mesh=mesh, in_specs=(row_spec, row_spec, expert_spec, expert_spec),
                          out_specs=row_spec, check_vma=False)

time: 92.5 us -> 82.7 us (0.89)
  Pallas kernels: 88 us -> 77.4 us
  other arithmetic: 0 us -> 3.11 us
  local copies, waits for them, and re-layouts: 3.49 us -> 1.19 us
    pallas_call x1, Pallas kernels: 88 us -> 77.4 us  [call(): pl.pallas_call(functools.partial(moe_kernel, cap, units), out_shape=(jax....]
    convert_element_type x0 -> x1, other arithmetic: none -> 3.11 us  [local_step(): return (x_rows.astype(F32) + mix).astype(BF16)]
    unnamed x1 -> x0, local copies, waits for them, and re-layouts: 2.3 us -> none
where the time goes in v3:
time: 82.7 us; the launch traced here: 82.5 us
  Pallas kernels  77.4 us (94%)
  other arithmetic  3.11 us (4%)
  local copies, waits for them, and re-layouts  1.19 us (1%)
    pallas_call x1, Pallas kernels, call(): pl.pallas_call(functools.partial(moe_kernel, cap, units), out_shape=(jax....  77.4 us
    convert_element_type x1, other arithmetic, local_step(): return (x_rows.astype(F32) + mix).astype(BF16)  3.11 us

profile of v3, /device:TPU:0, one launch (start us, length us, event | category | flops | bytes accessed | tf_op | source)
XLA Modules:
  0.0 82.5 jit_solution(12732132684121740153)
XLA Ops:
  0.0 77.4 %shard_map.46 = (f32[256,2048]{1,0:T(8,128)}, f32[8,128]{1,0:T(8,128)}) custom-call(bf16[256,2048]{1,0:T(8,128)(2,1)} %x_hbm.1, f32[64,256]{1,0:T(8,128)} %bitcast.2, bf16[16,2048,1408]{2,1,0:T(8,128)(2,1)} %w1_hbm.1, bf16[16,1408,2048]{2,1,0:T(8,128)(2,1)} %w2_hbm.1), custom_call_target="tpu_custom_call" | custom-call | tf_op jit(solution)/shard_map/pallas_call | solution.py:375
  77.4 1.2 %slice.3 = f32[1,1]{1,0:T(1,128)} slice(f32[8,128]{1,0:T(8,128)} %get-tuple-element.24), slice={[0:1], [0:1]} | slice | bytes 8 | tf_op jit(solution)/shard_map/slice | solution.py:388
  79.2 0.2 conditional.1
  79.4 3.1 %add_convert_fusion = bf16[256,2048]{1,0:T(8,128)(2,1)} fusion(f32[256,2048]{1,0:T(8,128)} %get-tuple-element.26, bf16[256,2048]{1,0:T(8,128)(2,1)} %x_hbm.1), kind=kLoop, calls=%fused_computation | loop fusion | flops 1572864 | bytes 4194304 | tf_op jit(solution)/shard_map/convert_element_type | solution.py:389

commit v4 on v3

--- a/solution.py
+++ b/solution.py
@@ -29,8 +29,8 @@
     return mask.astype(F32).astype(BF16)
 
 
-def moe_kernel(cap, units, x_hbm, lt_ref, w1_hbm, w2_hbm, out_ref, flag_ref, xall, st_own, st_all, dmat, xg, hacc, hb,
-               w1buf, w2buf, zs, pk, zr, meta_own, meta_in, flag_own, flag_in, choice, w1_sem, w2_sem, xl_sem, xs_sem,
+def moe_kernel(cap, units, x_hbm, lt_ref, w1_hbm, w2_hbm, out_ref, flag_ref, xall, st_own, st_all, dmat, xg, hacc, hb0, hb1,
+               w1buf, w2buf, zs, pk, zr, acc, meta_own, meta_in, flag_own, flag_in, choice, w1_sem, w2_sem, xl_sem, xs_sem,
                xr_sem, ss_sem, sr_sem, ms_sem, mr_sem, fs_sem, fr_sem, ps_sem, pr_sem, zs_sem, zr_sem):
     nexp, tok = lt_ref.shape
     edev, d_model, ff = w1_hbm.shape
@@ -199,9 +199,13 @@
     for r in (2, 3, 1):
         m_remote(r).start()
 
-    def gather_chunk(c):
+    def relay(c):
         x_remote(c, 2).wait_recv()
         x_remote(c, 3).start()
+
+    def gather_chunk(c):
+        if c < 2:
+            relay(c)
         x_remote(c, 1).wait_recv()
         for r in range(NREL):
             if r == 3:
@@ -213,6 +217,10 @@
         gather_chunk(c)
 
         def first_phase(j, carry):
+            if c > 0:
+                @pl.when(j == edev // STEP - 1)
+                def _():
+                    relay(c + 1)
             i0 = c * edev + j * STEP
             for q in range(STEP):
                 w1_copy(i0 + q).wait()
@@ -244,58 +252,77 @@
         choice[:, 0:1] = jnp.sum(jnp.where(is1, place, 0.0), axis=1, keepdims=True)
         choice[:, 1:2] = jnp.sum(jnp.where(is2, place, 0.0), axis=1, keepdims=True)
 
-    def second_phase(e, carry):
-        @pl.when(e == edev // 4)
+    def first_product(e, hidden):
+        h = hacc[e] + jnp.dot(xg[e].reshape(rows, ck), w1buf[(last + e) % NS1], preferred_element_type=F32)
+        hidden[...] = jax.nn.gelu(h, approximate=True).astype(BF16)
+
+    def send_packed(e):
+        start = sum((e > j).astype(jnp.int32) for j in range(edev - 1) if units[j]) * UNIT
+        start = pl.multiple_of(start, UNIT)
+        for r in (2, 3):
+            row = (iota((UNIT, slots), 0) + start).astype(F32)
+            pick = onehot(row == packed_row[r - 2])
+            for c in range(NCH):
+                cols = pl.ds(c * ck, ck)
+                pk[r - 2, pl.ds(start, UNIT), cols] = jnp.dot(pick, zs[r - 1, :, cols],
+                                                              preferred_element_type=F32).astype(BF16)
+        for r in (2, 3):
+            pack_remote(r, start, (start >= split).astype(jnp.int32)).start()
+
+    def expert(e, hidden, following):
+        if following is not None:
+            w1_copy(last + e + 1).wait()
+        w2_copy(e).wait()
+        if following is not None:
+            first_product(e + 1, following)
+        first = pl.multiple_of(e * src_cap, src_cap)
+        for c in range(NCH):
+            cols = pl.ds(c * ck, ck)
+            z = jnp.dot(hidden[...], w2buf[e % NS2, :, cols], preferred_element_type=F32).astype(BF16)
+            zr[0, pl.ds(first, src_cap), cols] = z[:src_cap]
+            for r in range(1, NREL):
+                zs[r - 1, pl.ds(first, src_cap), cols] = z[r * src_cap:(r + 1) * src_cap]
+
+        @pl.when(e + NS2 < edev)
+        def _():
+            w2_copy(e + NS2).start()
+
+        @pl.when(e + 1 + NS1 < edev)
+        def _():
+            w1_copy(last + e + 1 + NS1).start()
+
+        @pl.when(functools.reduce(jnp.logical_or, [e == j for j in range(edev) if units[j]]))
+        def _():
+            send_packed(e)
+        partner_remote(e).start()
+
+    w1_copy(last).wait()
+    first_product(0, hb0)
+    if NS1 < edev:
+        w1_copy(last + NS1).start()
+
+    def second_phase(j, carry):
+        @pl.when(j == 2)
         def _():
             place_rows()
 
-        @pl.when(e == edev // 2)
+        @pl.when(j == 4)
         def _():
             for k in range(1, ngroups):
                 f_remote(k).start()
-        w1_copy(last + e).wait()
-        h = hacc[e] + jnp.dot(xg[e].reshape(rows, ck), w1buf[(last + e) % NS1], preferred_element_type=F32)
-
-        @pl.when(e + NS1 < edev)
-        def _():
-            w1_copy(last + e + NS1).start()
-        hb[...] = jax.nn.gelu(h, approximate=True).astype(BF16)
-        w2_copy(e).wait()
-        first = pl.multiple_of(e * src_cap, src_cap)
-        for c in range(NCH):
-            cols = pl.ds(c * ck, ck)
-            z = jnp.dot(hb[...], w2buf[e % NS2, :, cols], preferred_element_type=F32).astype(BF16)
-            zr[0, pl.ds(first, src_cap), cols] = z[:src_cap]
-            for r in range(1, NREL):
-                zs[r - 1, pl.ds(first, src_cap), cols] = z[r * src_cap:(r + 1) * src_cap]
-
-        @pl.when(e + NS2 < edev)
-        def _():
-            w2_copy(e + NS2).start()
-
-        @pl.when(functools.reduce(jnp.logical_or, [e == j for j in range(edev) if units[j]]))
-        def _():
-            start = sum((e > j).astype(jnp.int32) for j in range(edev - 1) if units[j]) * UNIT
-            start = pl.multiple_of(start, UNIT)
-            for r in (2, 3):
-                row = (iota((UNIT, slots), 0) + start).astype(F32)
-                pick = onehot(row == packed_row[r - 2])
-                for c in range(NCH):
-                    cols = pl.ds(c * ck, ck)
-                    pk[r - 2, pl.ds(start, UNIT), cols] = jnp.dot(pick, zs[r - 1, :, cols],
-                                                                  preferred_element_type=F32).astype(BF16)
-            for r in (2, 3):
-                pack_remote(r, start, (start >= split).astype(jnp.int32)).start()
-        partner_remote(e).start()
+        expert(2 * j, hb0, hb1)
+        expert(2 * j + 1, hb1, hb0)
         return carry
-    lax.fori_loop(0, edev, second_phase, 0)
+    lax.fori_loop(0, edev // 2 - 1, second_phase, 0)
+    expert(jnp.int32(edev - 2), hb0, hb1)
+    expert(jnp.int32(edev - 1), hb1, None)
 
     for k in range(1, ngroups):
         f_remote(k).wait_recv()
     flag = flag_own[...]
     for k in range(1, ngroups):
         flag = jnp.maximum(flag, flag_in[k])
-    flag_ref[...] = flag
+    flag_ref[0] = (jnp.max(flag) > 0.0).astype(jnp.int32)
 
     slot1, slot2 = choice[:, 0:1], choice[:, 1:2]
     far = total_rows - split
@@ -315,8 +342,11 @@
             mix = (gate1 * jnp.dot(pick1, zc, preferred_element_type=F32)
                    + gate2 * jnp.dot(pick2, zc, preferred_element_type=F32))
             if n > 0:
-                mix = out_ref[:, cols] + mix
-            out_ref[:, cols] = mix
+                mix = acc[:, cols] + mix
+            if n < len(pieces) - 1:
+                acc[:, cols] = mix
+            else:
+                out_ref[:, cols] = (xall[0, c].astype(F32) + mix).astype(BF16)
 
     for k in range(1, ngroups):
         f_remote(k).wait_send()
@@ -354,12 +384,13 @@
             pltpu.VMEM((NREL, slots, tok), BF16),
             pltpu.VMEM((edev, NREL, src_cap, ck), BF16),
             pltpu.VMEM((edev, rows, ff), F32),
-            pltpu.VMEM((rows, ff), BF16),
+            pltpu.VMEM((rows, ff), BF16), pltpu.VMEM((rows, ff), BF16),
             pltpu.VMEM((NS1, ck, ff), BF16),
             pltpu.VMEM((NS2, ff, d_model), BF16),
             pltpu.VMEM((NREL - 1, slots, d_model), BF16),
             pltpu.VMEM((2, sum(units) * UNIT, d_model), BF16),
             pltpu.VMEM((NREL, slots, d_model), BF16),
+            pltpu.VMEM((tok, d_model), F32),
             pltpu.VMEM((NREL, 8, 128), F32), pltpu.VMEM((NREL, 8, 128), F32),
             pltpu.VMEM((8, 128), F32), pltpu.VMEM((ngroups, 8, 128), F32), pltpu.VMEM((tok, 128), F32),
             dma((NS1,)), dma((NS2,)), dma((NCH,)),
@@ -374,9 +405,9 @@
         hbm = pl.BlockSpec(memory_space=pl.ANY)
         return pl.pallas_call(
             functools.partial(moe_kernel, cap, units),
-            out_shape=(jax.ShapeDtypeStruct((tok, d_model), F32), jax.ShapeDtypeStruct((8, 128), F32)),
+            out_shape=(jax.ShapeDtypeStruct((tok, d_model), BF16), jax.ShapeDtypeStruct((1,), jnp.int32)),
             in_specs=[hbm, vmem, hbm, hbm],
-            out_specs=(vmem, vmem),
+            out_specs=(vmem, pl.BlockSpec(memory_space=pltpu.SMEM)),
             scratch_shapes=scratch,
             compiler_params=pltpu.CompilerParams(collective_id=collective, has_side_effects=True,
                                                  vmem_limit_bytes=67000000),
@@ -384,9 +415,8 @@
 
     def local_step(x_rows, logits, w_in, w_out):
         args = (x_rows, logits.T, w_in, w_out)
-        mix, flag = call(PACKED, 0, *args)
-        mix = lax.cond(flag[0, 0] > 0.0, lambda: call(FULL, 1, *args)[0], lambda: mix)
-        return (x_rows.astype(F32) + mix).astype(BF16)
+        out, flag = call(PACKED, 0, *args)
+        return lax.cond(flag[0] > 0, lambda: call(FULL, 1, *args)[0], lambda: out)
 
     return jax.shard_map(local_step, mesh=mesh, in_specs=(row_spec, row_spec, expert_spec, expert_spec),
                          out_specs=row_spec, check_vma=False)

time: 82.7 us -> 80.8 us (0.977)
  other arithmetic: 3.11 us -> 0 us
  local copies, waits for them, and re-layouts: 1.19 us -> 2.3 us
    convert_element_type x1 -> x0, other arithmetic: 3.11 us -> none  [local_step(): return (x_rows.astype(F32) + mix).astype(BF16)]
    unnamed x0 -> x1, local copies, waits for them, and re-layouts: none -> 2.3 us
    slice x1 -> x0, local copies, waits for them, and re-layouts: 1.19 us -> none  [local_step(): flag[0, 0] > 0.0]
where the time goes in v4:
time: 80.8 us; the launch traced here: 80.6 us
  Pallas kernels  77.4 us (96%)
  local copies, waits for them, and re-layouts  2.3 us (3%)
    pallas_call x1, Pallas kernels, call(): pl.pallas_call(functools.partial(moe_kernel, cap, units), out_shape=(jax....  77.4 us
    unnamed x1, local copies, waits for them, and re-layouts  2.3 us

profile of v4, /device:TPU:0, one launch (start us, length us, event | category | flops | bytes accessed | tf_op | source)
XLA Modules:
  0.0 80.6 jit_solution(3424332504177505194)
XLA Ops:
  0.0 77.4 %shard_map.48 = (bf16[256,2048]{1,0:T(8,128)(2,1)}, s32[1]{0:T(128)}) custom-call(bf16[256,2048]{1,0:T(8,128)(2,1)} %x_hbm.1, f32[64,256]{1,0:T(8,128)} %bitcast.2, bf16[16,2048,1408]{2,1,0:T(8,128)(2,1)} %w1_hbm.1, bf16[16,1408,2048]{2,1,0:T(8,128)(2,1)} %w2_hbm.1), custom_call_target="tpu_custom_call" | custom-call | tf_op jit(solution)/shard_map/pallas_call | solution.py:406
  78.0 0.3 conditional.1
  78.3 2.3 %copy.10 = bf16[256,2048]{1,0:T(8,128)(2,1)} copy(bf16[256,2048]{1,0:T(8,128)(2,1)} %get-tuple-element.26) | data formatting | bytes 2097152

commit v5 on v4

--- a/solution.py
+++ b/solution.py
@@ -15,10 +15,12 @@
 NS1 = 14
 NS2 = 3
 STEP = 4
+DEFER = 4
 UNIT = 16
 TAIL = 2
-PACKED = (0, 1, 1, 0, 1, 0, 1, 0, 1, 1, 1, 1, 1, 1, 1, 1)
-FULL = (1,) * 16
+PACKED = (0, 1, 1, 0, 1, 1, 0, 1, 0, 1, 1, 1, 0, 2, 0, 2)
+SENT_ROWS = 7 / 8
+FULL = (0, 2) * 8
 
 
 def iota(shape, dim):
@@ -29,12 +31,15 @@
     return mask.astype(F32).astype(BF16)
 
 
-def moe_kernel(cap, units, x_hbm, lt_ref, w1_hbm, w2_hbm, out_ref, flag_ref, xall, st_own, st_all, dmat, xg, hacc, hb0, hb1,
+def moe_kernel(cap, units, far_rows, x_hbm, lt_ref, w1_hbm, w2_hbm, out_ref, flag_ref, xall, xp, st_own, st_far, st_all, dmat, xg, xgl, hacc, hb0, hb1,
                w1buf, w2buf, zs, pk, zr, acc, meta_own, meta_in, flag_own, flag_in, choice, w1_sem, w2_sem, xl_sem, xs_sem,
                xr_sem, ss_sem, sr_sem, ms_sem, mr_sem, fs_sem, fr_sem, ps_sem, pr_sem, zs_sem, zr_sem):
     nexp, tok = lt_ref.shape
     edev, d_model, ff = w1_hbm.shape
     src_cap = xg.shape[2]
+    kmaj = edev - DEFER
+    nitems = edev * NCH
+    nmaj = kmaj * NCH
     slots = edev * src_cap
     ck = d_model // NCH
     rows = NREL * src_cap
@@ -52,7 +57,10 @@
                                             device_id={'ep': dev[r]}, device_id_type=MESH)
 
     def w1_copy(i):
-        c, e = i // edev, i % edev
+        i = jnp.int32(i)
+        late = (i >= nmaj).astype(jnp.int32)
+        c = (1 - late) * (i // kmaj) + late * ((i - nmaj) % NCH)
+        e = (1 - late) * (i % kmaj) + late * (kmaj + (i - nmaj) // NCH)
         k = pl.multiple_of(c * ck, ck)
         s = i % NS1
         return pltpu.make_async_copy(w1_hbm.at[e, pl.ds(k, ck), :], w1buf.at[s], w1_sem.at[s])
@@ -65,12 +73,17 @@
         return pltpu.make_async_copy(x_hbm.at[:, pl.ds(c * ck, ck)], xall.at[0, c], xl_sem.at[c])
 
     def x_remote(c, slot):
-        return remote(xall.at[2 if slot == 3 else 0, c], xall.at[slot, c], xs_sem.at[slot - 1, c],
-                      xr_sem.at[slot - 1, c], 2 if slot == 2 else 1)
+        if slot == 1:
+            src, dst = xall.at[0, c], xall.at[1, c]
+        else:
+            dst = xall.at[slot, c, pl.ds(0, far_rows), :]
+            src = xp.at[c] if slot == 2 else xall.at[2, c, pl.ds(0, far_rows), :]
+        return remote(src, dst, xs_sem.at[slot - 1, c], xr_sem.at[slot - 1, c], 2 if slot == 2 else 1)
 
     def s_remote(r):
         first = pl.multiple_of(dev[r] * edev, edev)
-        return remote(st_own.at[pl.ds(first, edev), :], st_all.at[r], ss_sem.at[r - 1], sr_sem.at[r - 1], r)
+        src = st_own if r == 1 else st_far
+        return remote(src.at[pl.ds(first, edev), :], st_all.at[r], ss_sem.at[r - 1], sr_sem.at[r - 1], r)
 
     def m_remote(r):
         return remote(meta_own.at[r], meta_in.at[r], ms_sem.at[r - 1], mr_sem.at[r - 1], r)
@@ -88,8 +101,8 @@
     def partner_all():
         return remote(zr.at[1], zr.at[1], ps_sem.at[0], pr_sem.at[0], 1)
 
-    def pack_remote(r, first, part):
-        return remote(pk.at[r - 2, pl.ds(first, UNIT), :], zr.at[r, pl.ds(first, UNIT), :], zs_sem.at[r - 2, part],
+    def pack_remote(r, first, size, part):
+        return remote(pk.at[r - 2, pl.ds(first, size), :], zr.at[r, pl.ds(first, size), :], zs_sem.at[r - 2, part],
                       zr_sem.at[r - 2, part], r)
 
     def pack_part(r, part):
@@ -115,6 +128,9 @@
     for r in (2, 3):
         zs[r - 1] = jnp.zeros(zs.shape[1:], BF16)
     meta_own[...] = jnp.zeros_like(meta_own)
+    if far_rows < tok:
+        for r in (2, 3):
+            xall[r, :, far_rows:, :] = jnp.zeros((NCH, tok - far_rows, ck), BF16)
 
     lt = lt_ref[...]
     m1t = jnp.max(lt, axis=0, keepdims=True)
@@ -122,13 +138,24 @@
     chosen_t = lt >= m2t
     upper = onehot(iota((tok, tok), 0) < iota((tok, tok), 1))
     before_t = jnp.dot(onehot(chosen_t), upper, preferred_element_type=F32)
-    st_own[...] = jnp.where(chosen_t, before_t, -1.0).astype(BF16)
+    slot_t = jnp.where(chosen_t, before_t + 1.0, 0.0).astype(BF16)
+    st_own[...] = slot_t
+    other = iota((nexp, tok), 0) // (2 * edev) == 1 - mx
+    need = jnp.max(jnp.where(jnp.logical_and(chosen_t, other), 1.0, 0.0), axis=0, keepdims=True)
+    order = jnp.dot(jnp.broadcast_to(need, (UNIT, tok)).astype(BF16), upper, preferred_element_type=F32)[0:1]
+    order = jnp.where(need > 0.0, order, -1.0)
+    row_no = iota((tok, tok), 0)
+    pack_x = onehot(jnp.logical_and(order == row_no.astype(F32), row_no < far_rows))
+    over = (jnp.sum(need, axis=1, keepdims=True) > float(far_rows)).astype(F32)
+    st_far[...] = lax.dot_general(slot_t, pack_x, (((1,), (1,)), ((), ())), preferred_element_type=F32).astype(BF16)
+    for c in range(NCH):
+        x_local(c).wait()
+        xp[c] = jnp.dot(pack_x[:far_rows], xall[0, c], preferred_element_type=F32).astype(BF16)
 
     pl.semaphore_wait(barrier, NREL - 1 + ngroups - 1)
     for r in (2, 3, 1):
         s_remote(r).start()
     for c in range(NCH):
-        x_local(c).wait()
         x_remote(c, 2).start()
         x_remote(c, 1).start()
 
@@ -147,7 +174,8 @@
     for r in range(1, NREL):
         s_remote(r).wait_recv()
     own_first = pl.multiple_of(me * edev, edev)
-    pos = [st_own[pl.ds(own_first, edev), :].astype(F32)] + [st_all[r].astype(F32) for r in range(1, NREL)]
+    pos = [st_own[pl.ds(own_first, edev), :].astype(F32) - 1.0]
+    pos += [st_all[r].astype(F32) - 1.0 for r in range(1, NREL)]
     cnt = [jnp.sum((p >= 0.0).astype(F32), axis=1, keepdims=True) for p in pos]
     ahead = []
     for r in range(NREL):
@@ -162,7 +190,6 @@
     exp_row = exp_no.astype(F32)
     wide = iota((edev, slots), 1)
     own_slot = wide // src_cap == iota((edev, slots), 0)
-    over = jnp.zeros((1, 1), F32)
     packed_row = [None, None]
     own_meta = None
     for r in range(NREL):
@@ -211,17 +238,19 @@
             if r == 3:
                 x_remote(c, 3).wait_recv()
             part = jnp.dot(dmat[r], xall[r, c], preferred_element_type=F32).astype(BF16)
-            xg[:, r] = part.reshape(edev, src_cap, ck)
+            part = part.reshape(edev, src_cap, ck)
+            xg[:, r] = part[:kmaj]
+            xgl[:, c, r] = part[kmaj:]
 
     for c in range(NCH - 1):
         gather_chunk(c)
 
         def first_phase(j, carry):
             if c > 0:
-                @pl.when(j == edev // STEP - 1)
+                @pl.when(j == kmaj // STEP - 1)
                 def _():
                     relay(c + 1)
-            i0 = c * edev + j * STEP
+            i0 = c * kmaj + j * STEP
             for q in range(STEP):
                 w1_copy(i0 + q).wait()
             for q in range(STEP):
@@ -233,9 +262,9 @@
             for q in range(STEP):
                 w1_copy(i0 + q + NS1).start()
             return carry
-        lax.fori_loop(0, edev // STEP, first_phase, 0)
-
-    last = (NCH - 1) * edev
+        lax.fori_loop(0, kmaj // STEP, first_phase, 0)
+
+    last = (NCH - 1) * kmaj
     gather_chunk(NCH - 1)
 
     def place_rows():
@@ -252,29 +281,39 @@
         choice[:, 0:1] = jnp.sum(jnp.where(is1, place, 0.0), axis=1, keepdims=True)
         choice[:, 1:2] = jnp.sum(jnp.where(is2, place, 0.0), axis=1, keepdims=True)
 
-    def first_product(e, hidden):
-        h = hacc[e] + jnp.dot(xg[e].reshape(rows, ck), w1buf[(last + e) % NS1], preferred_element_type=F32)
+    def w1_items(e, whole):
+        return [nmaj + (e - kmaj) * NCH + c for c in range(NCH)] if whole else [last + e]
+
+    def first_product(e, whole, hidden):
+        if whole:
+            h = None
+            for c, i in enumerate(w1_items(e, whole)):
+                part = jnp.dot(xgl[e - kmaj, c].reshape(rows, ck), w1buf[i % NS1], preferred_element_type=F32)
+                h = part if h is None else h + part
+        else:
+            h = hacc[e] + jnp.dot(xg[e].reshape(rows, ck), w1buf[(last + e) % NS1], preferred_element_type=F32)
         hidden[...] = jax.nn.gelu(h, approximate=True).astype(BF16)
 
-    def send_packed(e):
-        start = sum((e > j).astype(jnp.int32) for j in range(edev - 1) if units[j]) * UNIT
+    def send_packed(e, size):
+        start = sum((e > j).astype(jnp.int32) * units[j] for j in range(edev - 1) if units[j]) * UNIT
         start = pl.multiple_of(start, UNIT)
         for r in (2, 3):
-            row = (iota((UNIT, slots), 0) + start).astype(F32)
+            row = (iota((size, slots), 0) + start).astype(F32)
             pick = onehot(row == packed_row[r - 2])
             for c in range(NCH):
                 cols = pl.ds(c * ck, ck)
-                pk[r - 2, pl.ds(start, UNIT), cols] = jnp.dot(pick, zs[r - 1, :, cols],
+                pk[r - 2, pl.ds(start, size), cols] = jnp.dot(pick, zs[r - 1, :, cols],
                                                               preferred_element_type=F32).astype(BF16)
         for r in (2, 3):
-            pack_remote(r, start, (start >= split).astype(jnp.int32)).start()
-
-    def expert(e, hidden, following):
-        if following is not None:
-            w1_copy(last + e + 1).wait()
+            pack_remote(r, start, size, (start >= split).astype(jnp.int32)).start()
+
+    def expert(e, hidden, following, whole):
+        items = w1_items(e + 1, whole) if following is not None else []
+        for i in items:
+            w1_copy(i).wait()
         w2_copy(e).wait()
         if following is not None:
-            first_product(e + 1, following)
+            first_product(e + 1, whole, following)
         first = pl.multiple_of(e * src_cap, src_cap)
         for c in range(NCH):
             cols = pl.ds(c * ck, ck)
@@ -287,19 +326,20 @@
         def _():
             w2_copy(e + NS2).start()
 
-        @pl.when(e + 1 + NS1 < edev)
-        def _():
-            w1_copy(last + e + 1 + NS1).start()
-
-        @pl.when(functools.reduce(jnp.logical_or, [e == j for j in range(edev) if units[j]]))
-        def _():
-            send_packed(e)
+        for i in items:
+            @pl.when(i + NS1 < nitems)
+            def _():
+                w1_copy(i + NS1).start()
+
+        for n in set(units) - {0}:
+            @pl.when(functools.reduce(jnp.logical_or, [e == j for j in range(edev) if units[j] == n]))
+            def _():
+                send_packed(e, n * UNIT)
         partner_remote(e).start()
 
     w1_copy(last).wait()
-    first_product(0, hb0)
-    if NS1 < edev:
-        w1_copy(last + NS1).start()
+    first_product(0, False, hb0)
+    w1_copy(last + NS1).start()
 
     def second_phase(j, carry):
         @pl.when(j == 2)
@@ -310,12 +350,18 @@
         def _():
             for k in range(1, ngroups):
                 f_remote(k).start()
-        expert(2 * j, hb0, hb1)
-        expert(2 * j + 1, hb1, hb0)
+        expert(2 * j, hb0, hb1, False)
+        expert(2 * j + 1, hb1, hb0, False)
         return carry
-    lax.fori_loop(0, edev // 2 - 1, second_phase, 0)
-    expert(jnp.int32(edev - 2), hb0, hb1)
-    expert(jnp.int32(edev - 1), hb1, None)
+    lax.fori_loop(0, kmaj // 2 - 1, second_phase, 0)
+    expert(jnp.int32(kmaj - 2), hb0, hb1, False)
+
+    def third_phase(j, carry):
+        expert(kmaj - 1 + 2 * j, hb1, hb0, True)
+        expert(kmaj + 2 * j, hb0, hb1, True)
+        return carry
+    lax.fori_loop(0, DEFER // 2, third_phase, 0)
+    expert(jnp.int32(edev - 1), hb1, None, False)
 
     for k in range(1, ngroups):
         f_remote(k).wait_recv()
@@ -367,7 +413,7 @@
     row_spec = P(('dp', 'ep'), None)
     expert_spec = P('ep', None, None)
 
-    def call(units, collective, x_rows, logits_t, w_in, w_out):
+    def call(units, share, collective, x_rows, logits_t, w_in, w_out):
         tok, d_model = x_rows.shape
         nexp = logits_t.shape[0]
         edev, _, ff = w_in.shape
@@ -376,14 +422,18 @@
         slots = edev * src_cap
         rows = NREL * src_cap
         ck = d_model // NCH
+        far_rows = int(tok * share)
+        kmaj = edev - DEFER
         dma = pltpu.SemaphoreType.DMA
         scratch = [
             pltpu.VMEM((NREL, NCH, tok, ck), BF16),
-            pltpu.VMEM((nexp, tok), BF16),
+            pltpu.VMEM((NCH, far_rows, ck), BF16),
+            pltpu.VMEM((nexp, tok), BF16), pltpu.VMEM((nexp, tok), BF16),
             pltpu.VMEM((NREL, edev, tok), BF16),
             pltpu.VMEM((NREL, slots, tok), BF16),
-            pltpu.VMEM((edev, NREL, src_cap, ck), BF16),
-            pltpu.VMEM((edev, rows, ff), F32),
+            pltpu.VMEM((kmaj, NREL, src_cap, ck), BF16),
+            pltpu.VMEM((DEFER, NCH, NREL, src_cap, ck), BF16),
+            pltpu.VMEM((kmaj, rows, ff), F32),
             pltpu.VMEM((rows, ff), BF16), pltpu.VMEM((rows, ff), BF16),
             pltpu.VMEM((NS1, ck, ff), BF16),
             pltpu.VMEM((NS2, ff, d_model), BF16),
@@ -404,7 +454,7 @@
         vmem = pl.BlockSpec(memory_space=pltpu.VMEM)
         hbm = pl.BlockSpec(memory_space=pl.ANY)
         return pl.pallas_call(
-            functools.partial(moe_kernel, cap, units),
+            functools.partial(moe_kernel, cap, units, far_rows),
             out_shape=(jax.ShapeDtypeStruct((tok, d_model), BF16), jax.ShapeDtypeStruct((1,), jnp.int32)),
             in_specs=[hbm, vmem, hbm, hbm],
             out_specs=(vmem, pl.BlockSpec(memory_space=pltpu.SMEM)),
@@ -415,8 +465,8 @@
 
     def local_step(x_rows, logits, w_in, w_out):
         args = (x_rows, logits.T, w_in, w_out)
-        out, flag = call(PACKED, 0, *args)
-        return lax.cond(flag[0] > 0, lambda: call(FULL, 1, *args)[0], lambda: out)
+        out, flag = call(PACKED, SENT_ROWS, 0, *args)
+        return lax.cond(flag[0] > 0, lambda: call(FULL, 1, 1, *args)[0], lambda: out)
 
     return jax.shard_map(local_step, mesh=mesh, in_specs=(row_spec, row_spec, expert_spec, expert_spec),
                          out_specs=row_spec, check_vma=False)

time: 80.8 us -> 76.9 us (0.952)
  Pallas kernels: 77.4 us -> 73.6 us
    pallas_call x1, Pallas kernels: 77.4 us -> 73.6 us  [call(): pl.pallas_call(functools.partial(moe_kernel, cap, units, far_rows), out_s...]
where the time goes in v5:
time: 76.9 us; the launch traced here: 76.7 us
  Pallas kernels  73.6 us (96%)
  local copies, waits for them, and re-layouts  2.3 us (3%)
    pallas_call x1, Pallas kernels, call(): pl.pallas_call(functools.partial(moe_kernel, cap, units, far_rows), out_s...  73.6 us
    unnamed x1, local copies, waits for them, and re-layouts  2.3 us

profile of v5, /device:TPU:0, one launch (start us, length us, event | category | flops | bytes accessed | tf_op | source)
XLA Modules:
  0.0 76.7 jit_solution(9170098060348686350)
XLA Ops:
  0.0 73.6 %shard_map.48 = (bf16[256,2048]{1,0:T(8,128)(2,1)}, s32[1]{0:T(128)}) custom-call(bf16[256,2048]{1,0:T(8,128)(2,1)} %x_hbm.1, f32[64,256]{1,0:T(8,128)} %bitcast.2, bf16[16,2048,1408]{2,1,0:T(8,128)(2,1)} %w1_hbm.1, bf16[16,1408,2048]{2,1,0:T(8,128)(2,1)} %w2_hbm.1), custom_call_target="tpu_custom_call" | custom-call | tf_op jit(solution)/shard_map/pallas_call | solution.py:456
  74.2 0.3 conditional.1
  74.4 2.3 %copy.10 = bf16[256,2048]{1,0:T(8,128)(2,1)} copy(bf16[256,2048]{1,0:T(8,128)(2,1)} %get-tuple-element.26) | data formatting | bytes 2097152

commit v6 on v5

--- a/solution.py
+++ b/solution.py
@@ -455,12 +455,12 @@
         hbm = pl.BlockSpec(memory_space=pl.ANY)
         return pl.pallas_call(
             functools.partial(moe_kernel, cap, units, far_rows),
-            out_shape=(jax.ShapeDtypeStruct((tok, d_model), BF16), jax.ShapeDtypeStruct((1,), jnp.int32)),
+            out_shape=(pltpu.VMEM((tok, d_model), BF16), pltpu.SMEM((1,), jnp.int32)),
             in_specs=[hbm, vmem, hbm, hbm],
             out_specs=(vmem, pl.BlockSpec(memory_space=pltpu.SMEM)),
             scratch_shapes=scratch,
             compiler_params=pltpu.CompilerParams(collective_id=collective, has_side_effects=True,
-                                                 vmem_limit_bytes=67000000),
+                                                 vmem_limit_bytes=65900000),
         )(x_rows, logits_t, w_in, w_out)
 
     def local_step(x_rows, logits, w_in, w_out):

time: 76.9 us -> 74.1 us (0.964)
  local copies, waits for them, and re-layouts: 2.3 us -> 0.98 us
  Pallas kernels: 73.6 us -> 72.7 us
    unnamed x1 -> x3, local copies, waits for them, and re-layouts: 2.3 us -> 0.98 us
    pallas_call x1, Pallas kernels: 73.6 us -> 72.7 us  [call(): pl.pallas_call(functools.partial(moe_kernel, cap, units, far_rows), out_s...]
where the time goes in v6:
time: 74.1 us; the launch traced here: 73.9 us
  Pallas kernels  72.7 us (98%)
  local copies, waits for them, and re-layouts  0.98 us (1%)
    pallas_call x1, Pallas kernels, call(): pl.pallas_call(functools.partial(moe_kernel, cap, units, far_rows), out_s...  72.7 us

profile of v6, /device:TPU:0, one launch (start us, length us, event | category | flops | bytes accessed | tf_op | source)
XLA Modules:
  0.0 73.9 jit_solution(556637752600987114)
XLA Ops:
  0.0 0.0 copy-start
  0.0 72.7 %shard_map.48 = (bf16[256,2048]{1,0:T(8,128)(2,1)S(1)}, s32[1]{0:T(128)S(4)}) custom-call(bf16[256,2048]{1,0:T(8,128)(2,1)} %x_hbm.1, f32[64,256]{1,0:T(8,128)} %bitcast.2, bf16[16,2048,1408]{2,1,0:T(8,128)(2,1)} %w1_hbm.1, bf16[16,1408,2048]{2,1,0:T(8,128)(2,1)} %w2_hbm.1), custom_call_target="tpu_custom_call" | custom-call | tf_op jit(solution)/shard_map/pallas_call | solution.py:456
  72.7 0.0 copy-done
  72.7 0.3 conditional.1
  73.0 1.0 %copy.10 = bf16[256,2048]{1,0:T(8,128)(2,1)} copy(bf16[256,2048]{1,0:T(8,128)(2,1)S(1)} %get-tuple-element.26) | data formatting | bytes 2097152
Async XLA Ops:
  0.0 72.7 %copy-start = (f32[256,64]{0,1:T(8,128)S(1)}, f32[256,64]{0,1:T(8,128)}, u32[]{:S(2)}) copy-start(f32[256,64]{0,1:T(8,128)} %param.7) | copy-start | bytes 196612

commit v7 on v6

--- a/solution.py
+++ b/solution.py
@@ -18,7 +18,7 @@
 DEFER = 4
 UNIT = 16
 TAIL = 2
-PACKED = (0, 1, 1, 0, 1, 1, 0, 1, 0, 1, 1, 1, 0, 2, 0, 2)
+PACKED = (0, 1, 1, 0, 1, 1, 0, 1, 0, 1, 1, 1, 1, 1, 0, 2)
 SENT_ROWS = 7 / 8
 FULL = (0, 2) * 8
 

time: 74.1 us -> 72.8 us (0.982)
  Pallas kernels: 72.7 us -> 71.4 us
    pallas_call x1, Pallas kernels: 72.7 us -> 71.4 us  [call(): pl.pallas_call(functools.partial(moe_kernel, cap, units, far_rows), out_s...]
where the time goes in v7:
time: 72.8 us; the launch traced here: 72.7 us
  Pallas kernels  71.4 us (98%)
  local copies, waits for them, and re-layouts  0.98 us (1%)
    pallas_call x1, Pallas kernels, call(): pl.pallas_call(functools.partial(moe_kernel, cap, units, far_rows), out_s...  71.4 us

profile of v7, /device:TPU:0, one launch (start us, length us, event | category | flops | bytes accessed | tf_op | source)
XLA Modules:
  0.0 72.7 jit_solution(12964433409811086742)
XLA Ops:
  0.0 0.0 copy-start
  0.0 71.4 %shard_map.48 = (bf16[256,2048]{1,0:T(8,128)(2,1)S(1)}, s32[1]{0:T(128)S(4)}) custom-call(bf16[256,2048]{1,0:T(8,128)(2,1)} %x_hbm.1, f32[64,256]{1,0:T(8,128)} %bitcast.2, bf16[16,2048,1408]{2,1,0:T(8,128)(2,1)} %w1_hbm.1, bf16[16,1408,2048]{2,1,0:T(8,128)(2,1)} %w2_hbm.1), custom_call_target="tpu_custom_call" | custom-call | tf_op jit(solution)/shard_map/pallas_call | solution.py:456
  71.4 0.0 copy-done
  71.5 0.3 conditional.1
  71.7 1.0 %copy.10 = bf16[256,2048]{1,0:T(8,128)(2,1)} copy(bf16[256,2048]{1,0:T(8,128)(2,1)S(1)} %get-tuple-element.26) | data formatting | bytes 2097152
Async XLA Ops:
  0.0 71.4 %copy-start = (f32[256,64]{0,1:T(8,128)S(1)}, f32[256,64]{0,1:T(8,128)}, u32[]{:S(2)}) copy-start(f32[256,64]{0,1:T(8,128)} %param.7) | copy-start | bytes 196612
